TPU v7x, 32 devices: a whole 2x2x4 slice. The times are simulated.
32 devices in a mesh: seq: 8 (over z, y), grp: 4 (over x, core).
Axes of the slice: x: 2, y: 2, z: 4, core: 2. Of those that a mesh axis runs over, the one named last changes fastest.
Arguments:
- hidden: bfloat16 [256, 8192], P('grp', 'seq'), may hold values from -6 to 6
- w_qkv: bfloat16 [8192, 10240], P('seq', 'grp'), may hold values from -0.0625 to 0.0625
- b_qkv: float32 [10240], P('grp'), may hold values from -3 to 3
- w_out: bfloat16 [8192, 8192], P('seq', 'grp'), may hold values from -0.0625 to 0.0625
- k_cache: bfloat16 [4, 32768, 1024], P('grp', 'seq'), may hold values from -600 to 600
- v_cache: bfloat16 [4, 32768, 1024], P('grp', 'seq'), may hold values from -6 to 6
- lengths: int32 [256], replicated, may hold values from 1 to 16384, as said below
- page_table: int32 [256, 128], replicated, may hold values from -1 to 255, as said below
- positions: int32 [3, 256], replicated, may hold values from 0 to 4095
- group_of: int32 [256], replicated, may hold values from 0 to 3, as said below
Outputs:
- mixed: bfloat16 [256, 8192], P('seq', 'grp')
Inputs may be any that keep to these rules, and one draw needn't show every extreme that they name: `group_of`: each group serves exactly 64 requests. `lengths`: each group has a request of exactly 16384 cached positions. `page_table`: entry j of row r is the page of request r's group pool (page p lies on that group's device p // 32 of seq) that holds its positions j * 128 to (j + 1) * 128 - 1, for j < ceil(lengths[r] / 128); later entries are -1; no page belongs to two requests.
All inputs are finite; a program needn't handle non-finite values.
Results may differ from a plain program's by a relative error of at most 0.015.
The roundings to bfloat16 on the way count: a program that leaves them out, or rounds other values in their place, can miss the bound.
Values may be sent and summed in bfloat16 or wider, within the bound.
A program may use at most 128 MiB of HBM per device.

v0:
```python
import functools
import math

import jax
import jax.numpy as jnp
from jax import lax
from jax.experimental import pallas as pl
from jax.experimental.pallas import tpu as pltpu
from jax.sharding import PartitionSpec as P

HQ = 64
KVH = 8
HD = 128
PAGE = 128


rope_base = 1000000.0
neg_fill = -1e30


def rotate_heads(values, places, col_start, head_dim, turned):
    row_count, col_count = values.shape
    columns = col_start + jnp.arange(col_count, dtype=jnp.int32)
    within = columns % head_dim
    freq_index = within % (head_dim // 2)
    inverse_freq = jnp.exp(freq_index.astype(jnp.float32) * (-2.0 * math.log(rope_base) / head_dim))
    section = jnp.where(
        freq_index < head_dim // 8,
        0,
        jnp.where(freq_index < head_dim // 8 + 3 * head_dim // 16, 1, 2),
    )
    place_float = places.astype(jnp.float32)
    chosen = jnp.where(
        section[None, :] == 0,
        place_float[0][:, None],
        jnp.where(section[None, :] == 1, place_float[1][:, None], place_float[2][:, None]),
    )
    angles = chosen * inverse_freq[None, :]
    half = head_dim // 2
    partner = jnp.where(
        (within < half)[None, :], -jnp.roll(values, -half, axis=1), jnp.roll(values, half, axis=1)
    )
    rotated = values * jnp.cos(angles) + partner * jnp.sin(angles)
    return jnp.where((columns < turned)[None, :], rotated, values)


def attend_pages(block_pages, owner_ref, live_ref, rows_ref, key_ref, value_ref, out_ref, stat_ref):
    step = pl.program_id(0)
    group_q = HQ // KVH
    width = KVH * HD

    @pl.when(step == 0)
    def _():
        out_ref[...] = jnp.zeros_like(out_ref)
        lanes = lax.broadcasted_iota(jnp.int32, stat_ref.shape, 2)
        stat_ref[...] = jnp.where(lanes < HD // 2, neg_fill, 0.0)

    row_head = lax.broadcasted_iota(jnp.int32, (HQ, width), 0) // group_q
    col_head = lax.broadcasted_iota(jnp.int32, (HQ, width), 1) // HD
    own_head = (row_head == col_head).astype(jnp.float32).astype(jnp.bfloat16)
    place = lax.broadcasted_iota(jnp.int32, (HQ, PAGE), 1)
    lane = lax.broadcasted_iota(jnp.int32, (HQ, HD), 1)
    pages = []
    for j in range(block_pages):
        owner = owner_ref[step * block_pages + j]
        alive = place < live_ref[step * block_pages + j]
        query = rows_ref[owner, :HQ, :]
        spread = jnp.concatenate([query] * KVH, axis=1) * own_head
        keys = key_ref[0, j * PAGE : (j + 1) * PAGE, :]
        values = value_ref[0, j * PAGE : (j + 1) * PAGE, :]
        scores = lax.dot_general(
            spread, keys, (((1,), (1,)), ((), ())), preferred_element_type=jnp.float32
        ) * (HD**-0.5)
        scores = jnp.where(alive, scores, neg_fill)
        page_max = jnp.max(scores, axis=1, keepdims=True)
        weights = jnp.where(alive, jnp.exp(scores - page_max), 0.0)
        page_total = jnp.sum(weights, axis=1, keepdims=True)
        wide = jnp.dot(weights.astype(jnp.bfloat16), values, preferred_element_type=jnp.float32)
        page_out = jnp.concatenate(
            [
                wide[h * group_q : (h + 1) * group_q, h * HD : (h + 1) * HD]
                for h in range(KVH)
            ],
            axis=0,
        )
        pages.append((owner, page_max, page_total, page_out))
    for owner, page_max, page_total, page_out in pages:
        stat = stat_ref[owner]
        old_max = stat[:, :1]
        new_max = jnp.maximum(old_max, page_max)
        kept = jnp.exp(old_max - new_max)
        added = jnp.exp(page_max - new_max)
        out_ref[owner] = out_ref[owner] * kept + page_out * added
        total = stat[:, HD // 2 : HD // 2 + 1] * kept + page_total * added
        stat_ref[owner] = jnp.where(lane < HD // 2, new_max, total)


def local_attention(owner, live, rows, k_cache, v_cache):
    group_size = rows.shape[0]
    pool_pages = k_cache.shape[1] // PAGE
    block_pages = math.gcd(pool_pages, 4)
    cache_spec = pl.BlockSpec((1, block_pages * PAGE, KVH * HD), lambda i, *_: (0, i, 0))
    whole_spec = pl.BlockSpec((group_size, HQ, HD), lambda i, *_: (0, 0, 0))
    shape = jax.ShapeDtypeStruct((group_size, HQ, HD), jnp.float32)
    return pl.pallas_call(
        functools.partial(attend_pages, block_pages),
        grid_spec=pltpu.PrefetchScalarGridSpec(
            num_scalar_prefetch=2,
            grid=(pool_pages // block_pages,),
            in_specs=[
                pl.BlockSpec(rows.shape, lambda i, *_: (0, 0, 0)),
                cache_spec,
                cache_spec,
            ],
            out_specs=[whole_spec, whole_spec],
        ),
        out_shape=[shape, shape],
        compiler_params=pltpu.CompilerParams(
            dimension_semantics=("arbitrary",), vmem_limit_bytes=58 * 1024 * 1024
        ),
        cost_estimate=pl.CostEstimate(
            flops=4 * pool_pages * HQ * PAGE * KVH * HD,
            bytes_accessed=4 * pool_pages * PAGE * KVH * HD,
            transcendentals=pool_pages * HQ * PAGE,
        ),
    )(owner, live, rows, k_cache, v_cache)


def shards(hidden, w_qkv, b_qkv, w_out, k_cache, v_cache, lengths, page_table, positions, group_of):
    seq_count = lax.axis_size("seq")
    grp_count = lax.axis_size("grp")
    seq_index = lax.axis_index("seq")
    grp_index = lax.axis_index("grp")
    request_total = group_of.shape[0]
    group_size = request_total // grp_count
    share = group_size // seq_count
    col_count = w_qkv.shape[1]
    col_start = grp_index * col_count
    turned = (HQ + KVH) * HD
    group_q = HQ // KVH
    score_scale = HD ** (-0.5)
    request_ids = jnp.arange(request_total, dtype=jnp.int32)
    before = (group_of[None, :] < group_of[:, None]) | (group_of[None, :] == group_of[:, None]) & (
        request_ids[None, :] < request_ids[:, None]
    )
    restore = jnp.sum(before.astype(jnp.int32), axis=1)
    placed_at = restore[None, :] == request_ids[:, None]
    served_order = jnp.sum(jnp.where(placed_at, request_ids[None, :], 0), axis=1)
    served_ids = lax.dynamic_slice_in_dim(served_order, grp_index * group_size, group_size, 0)
    send_order = (
        served_order.reshape(grp_count, seq_count, share).transpose(1, 0, 2).reshape(request_total)
    )
    hidden_all = lax.all_gather(hidden, "grp", axis=0, tiled=True)[send_order]
    partial_sum = jnp.dot(hidden_all, w_qkv, preferred_element_type=jnp.float32)
    row_share = request_total // seq_count
    summed = jnp.sum(
        lax.all_to_all(
            partial_sum.reshape(seq_count, row_share, col_count),
            "seq",
            split_axis=0,
            concat_axis=0,
            tiled=True,
        ),
        axis=0,
    )
    my_rows = lax.dynamic_slice_in_dim(send_order, seq_index * row_share, row_share, 0)
    fresh_rows = rotate_heads(
        summed + b_qkv[None, :], positions[:, my_rows], col_start, HD, turned
    ).astype(jnp.bfloat16)
    outgoing = fresh_rows.reshape(grp_count, share, col_count)
    incoming = lax.all_to_all(outgoing, "grp", split_axis=0, concat_axis=2, tiled=True)
    head_rows = incoming.reshape(share, grp_count * col_count // HD, HD)
    rows = lax.all_to_all(
        jnp.broadcast_to(head_rows[None], (seq_count,) + head_rows.shape),
        "seq",
        split_axis=0,
        concat_axis=0,
        tiled=True,
    ).reshape((group_size,) + head_rows.shape[1:])

    served_len = lengths[served_ids]
    served_table = page_table[served_ids]
    most_pages = page_table.shape[1]
    page_counts = (served_len + PAGE - 1) // PAGE
    logical = jnp.arange(most_pages, dtype=jnp.int32)
    pool_pages = k_cache.shape[1] // PAGE
    local_page = served_table - seq_index * pool_pages
    usable = (
        (logical[None, :] < page_counts[:, None]) & (local_page >= 0) & (local_page < pool_pages)
    )
    pool_ids = jnp.arange(pool_pages, dtype=jnp.int32)
    matched = usable[:, :, None] & (local_page[:, :, None] == pool_ids[None, None, :])
    owner_ids = jnp.arange(group_size, dtype=jnp.int32)
    left = served_len[:, None] - logical[None, :] * PAGE
    live = jnp.max(jnp.where(matched, left[:, :, None], 0), axis=(0, 1))
    owner = jnp.max(jnp.where(matched, owner_ids[:, None, None], 0), axis=(0, 1))
    local_out, local_stat = local_attention(owner, live, rows, k_cache, v_cache)

    head_share = HQ // seq_count
    head_start = seq_index * head_share
    kv_share = max(1, head_share // group_q)
    kv_start = head_start // group_q
    query_here = lax.dynamic_slice_in_dim(rows, head_start, head_share, 1).astype(jnp.float32)
    key_here = lax.dynamic_slice_in_dim(rows, HQ + kv_start, kv_share, 1).astype(jnp.float32)
    value_here = lax.dynamic_slice_in_dim(rows, HQ + KVH + kv_start, kv_share, 1).astype(
        jnp.float32
    )
    key_here = jnp.repeat(key_here, head_share // kv_share, axis=1)
    value_here = jnp.repeat(value_here, head_share // kv_share, axis=1)
    new_here = jnp.sum(query_here * key_here, axis=2) * score_scale

    out_parts = lax.all_to_all(
        local_out.astype(jnp.bfloat16)
        .reshape(group_size, seq_count, head_share * HD)
        .transpose(1, 0, 2),
        "seq",
        split_axis=0,
        concat_axis=0,
        tiled=True,
    )
    stats = jnp.stack([local_stat[:, :, 0], local_stat[:, :, HD // 2]], axis=0)
    stats = stats.reshape(2, group_size, seq_count, head_share).transpose(2, 0, 1, 3)
    stat_parts = lax.all_to_all(
        stats.reshape(seq_count, 2 * group_size * head_share),
        "seq",
        split_axis=0,
        concat_axis=0,
        tiled=True,
    ).reshape(seq_count, 2, group_size, head_share)
    part_max = stat_parts[:, 0]
    part_total = stat_parts[:, 1]
    peak_here = jnp.maximum(jnp.max(part_max, axis=0), new_here)
    factor = jnp.exp(part_max - peak_here[None])
    fresh_weight = jnp.exp(new_here - peak_here)
    denominator = jnp.sum(part_total * factor, axis=0) + fresh_weight

    def widen(small):
        return jnp.repeat(small, HD, axis=-1)

    numerator = jnp.sum(out_parts.astype(jnp.float32) * widen(factor), axis=0) + widen(
        fresh_weight
    ) * value_here.reshape(group_size, head_share * HD)
    attended = (numerator / widen(denominator)).astype(jnp.bfloat16)
    gathered = lax.all_gather(attended, "grp", axis=0, tiled=True)
    by_request = gathered[restore]
    mixed = jnp.dot(by_request, w_out, preferred_element_type=jnp.float32).astype(jnp.bfloat16)
    mixed_parts = lax.all_to_all(
        mixed.reshape(seq_count, row_share, mixed.shape[1]),
        "seq",
        split_axis=0,
        concat_axis=0,
        tiled=True,
    )
    return jnp.sum(mixed_parts.astype(jnp.float32), axis=0).astype(jnp.bfloat16)


def solution(mesh):
    placed = (
        P("grp", "seq"),
        P("seq", "grp"),
        P("grp"),
        P("seq", "grp"),
        P("grp", "seq", None),
        P("grp", "seq", None),
        P(),
        P(),
        P(),
        P(),
    )
    return jax.shard_map(
        shards, mesh=mesh, in_specs=placed, out_specs=P("seq", "grp"), check_vma=False
    )
```

profile of v0, /device:TPU:0, one launch (start us, length us, event | category | flops | bytes accessed | tf_op | source)
XLA Modules:
  0.0 241.5 jit_solution(17532401085884404227)
XLA Ops:
  0.0 0.9 convert_reduce_fusion
  1.3 8.9 %all_gather.6 = bf16[256,1024]{1,0:T(8,128)(2,1)S(1)} all-gather(bf16[64,1024]{1,0:T(8,128)(2,1)} %param.10), channel_id=1, replica_groups=mesh['seq'=8,'grp'=4] {'grp'}, dimensions={0}, use_global_device_ids=true | all-gather | bytes 655360 | tf_op jit(solution)/shard_map/all_gather | solution.py:153
  10.2 1.2 gather_fusion.2
  11.3 5.5 %fusion.25 = f32[256,2560]{1,0:T(8,128)} fusion(bf16[256,1024]{1,0:T(8,128)(2,1)S(1)} %gather_fusion.2, bf16[1024,2560]{1,0:T(8,128)(2,1)} %param.11), kind=kOutput, calls=%fused_computation.90 | convolution fusion | flops 1342177280 | bytes 8388608 | tf_op jit(solution)/shard_map/dot_general | solution.py:154
  16.8 6.0 %all-to-all-start = ((f32[8,32,2560]{2,1,0:T(8,128)}), f32[8,32,2560]{2,1,0:T(8,128)S(1)}, u32[]{:S(2)}, u32[]{:S(2)}) async-start(f32[8,32,2560]{2,1,0:T(8,128)} %bitcast.68), calls=%async_computation | async-start | bytes 5242880 | tf_op jit(solution)/shard_map/all_to_all | solution.py:157
  24.3 58.5 %all-to-all-done = f32[8,32,2560]{2,1,0:T(8,128)S(1)} async-done(((f32[8,32,2560]{2,1,0:T(8,128)}), f32[8,32,2560]{2,1,0:T(8,128)S(1)}, u32[]{:S(2)}, u32[]{:S(2)}) %all-to-all-start) | async-done | bytes 2621472 | tf_op jit(solution)/shard_map/all_to_all | solution.py:157
  83.2 1.5 fusion.5
  84.8 7.3 %all_to_all.45 = bf16[4,8,2560]{2,1,0:T(8,128)(2,1)S(1)} all-to-all(bf16[4,8,2560]{2,1,0:T(8,128)(2,1)S(1)} %fusion.5), channel_id=1, replica_groups=mesh['seq'=8,'grp'=4] {'grp'}, dimensions={0} | all-to-all | bytes 327680 | tf_op jit(solution)/shard_map/all_to_all | solution.py:171
  92.3 1.2 broadcast_in_dim.174
  93.5 3.6 %all-to-all-start.2 = ((bf16[8,8,80,128]{3,2,1,0:T(8,128)(2,1)}), bf16[8,8,80,128]{3,2,1,0:T(8,128)(2,1)S(1)}, u32[]{:S(2)}, u32[]{:S(2)}) async-start(bf16[8,8,80,128]{3,2,1,0:T(8,128)(2,1)} %broadcast_in_dim.174), calls=%async_computation.2 | async-start | bytes 2621440 | tf_op jit(solution)/shard_map/all_to_all | solution.py:173
  98.8 1.1 select_reduce_fusion
  99.9 28.8 %all-to-all-done.2 = bf16[8,8,80,128]{3,2,1,0:T(8,128)(2,1)S(1)} async-done(((bf16[8,8,80,128]{3,2,1,0:T(8,128)(2,1)}), bf16[8,8,80,128]{3,2,1,0:T(8,128)(2,1)S(1)}, u32[]{:S(2)}, u32[]{:S(2)}) %all-to-all-start.2) | async-done | bytes 1310752 | tf_op jit(solution)/shard_map/all_to_all | solution.py:173
  128.8 1.1 copy-done.2
  129.8 20.5 %shard_map.100 = (f32[64,64,128]{2,1,0:T(8,128)}, f32[64,64,128]{2,1,0:T(8,128)}) custom-call(s32[32]{0:T(128)} %get-tuple-element.10.owner_ref, s32[32]{0:T(128)} %get-tuple-element.9.live_ref, bf16[64,80,128]{2,1,0:T(8,128)(2,1)} %bitcast.65, bf16[1,4096,1024]{2,1,0:T(8,128)(2,1)} %key_ref.1, bf16[1,4096,1024]{2,1,0:T(8,128)(2,1)} %value_ref.1), custom_call_target="tpu_custom_call" | custom-call | flops 1073741824 | bytes 16777216 | tf_op jit(solution)/shard_map/pallas_call | solution.py:105
  150.3 4.4 %fusion.24 = (f32[64,64,1]{2,1,0:T(8,128)}, f32[64,64,1]{2,1,0:T(8,128)S(1)}) fusion(f32[64,64,128]{2,1,0:T(8,128)} %get-tuple-element.8), kind=kLoop, calls=%fused_computation.89 | loop fusion | bytes 65536 | tf_op jit(solution)/shard_map/slice | solution.py:221
  154.7 2.6 %copy.45 = f32[64,64,1]{0,1,2:T(8,128)S(1)} copy(f32[64,64,1]{2,1,0:T(8,128)} %get-tuple-element.20) | data formatting | bytes 32768 | tf_op jit(solution)/shard_map/slice | solution.py:221
  157.3 1.2 copy.46
  158.7 0.9 all_to_all.38
  159.6 3.6 %all-to-all-start.4 = ((f32[8,1,1024]{2,1,0:T(1,128)}), f32[8,1,1024]{2,1,0:T(1,128)S(1)}, u32[]{:S(2)}, u32[]{:S(2)}) async-start(f32[8,1,1024]{2,1,0:T(1,128)} %all_to_all.38), calls=%async_computation.4 | async-start | bytes 65536 | tf_op jit(solution)/shard_map/all_to_all | solution.py:223
  163.2 1.8 convert_element_type.48
  165.5 1.6 copy.56
  167.1 2.8 %all-to-all-done.4 = f32[8,1,1024]{2,1,0:T(1,128)S(1)} async-done(((f32[8,1,1024]{2,1,0:T(1,128)}), f32[8,1,1024]{2,1,0:T(1,128)S(1)}, u32[]{:S(2)}, u32[]{:S(2)}) %all-to-all-start.4) | async-done | bytes 32800 | tf_op jit(solution)/shard_map/all_to_all | solution.py:223
  169.9 3.7 %all-to-all-start.3 = ((bf16[8,64,1024]{2,1,0:T(8,128)(2,1)}), bf16[8,64,1024]{2,1,0:T(8,128)(2,1)S(1)}, u32[]{:S(2)}, u32[]{:S(2)}) async-start(bf16[8,64,1024]{2,1,0:T(8,128)(2,1)} %bitcast.64), calls=%async_computation.3 | async-start | bytes 2097152 | tf_op jit(solution)/shard_map/all_to_all | solution.py:212
  173.7 1.6 dynamic-slice_convert_fusion
  175.4 1.0 multiply_reduce_fusion.1
  176.9 2.0 broadcast_in_dim.175
  178.9 1.7 reshape.291
  182.1 16.6 %all-to-all-done.3 = bf16[8,64,1024]{2,1,0:T(8,128)(2,1)S(1)} async-done(((bf16[8,64,1024]{2,1,0:T(8,128)(2,1)}), bf16[8,64,1024]{2,1,0:T(8,128)(2,1)S(1)}, u32[]{:S(2)}, u32[]{:S(2)}) %all-to-all-start.3) | async-done | bytes 1048608 | tf_op jit(solution)/shard_map/all_to_all | solution.py:212
  199.7 6.5 %all_gather.7 = bf16[256,1024]{1,0:T(8,128)(2,1)S(1)} all-gather(bf16[64,1024]{1,0:T(8,128)(2,1)S(1)} %fusion.6), channel_id=1, replica_groups=mesh['seq'=8,'grp'=4] {'grp'}, dimensions={0}, use_global_device_ids=true | all-gather | bytes 655360 | tf_op jit(solution)/shard_map/all_gather | solution.py:244
  206.2 1.2 gather_fusion.4
  207.4 3.4 %convolution_convert_fusion = bf16[256,2048]{1,0:T(8,128)(2,1)S(1)} fusion(bf16[256,1024]{1,0:T(8,128)(2,1)S(1)} %gather_fusion.4, bf16[1024,2048]{1,0:T(8,128)(2,1)} %param.13), kind=kOutput, calls=%fused_computation.5 | convolution fusion | flops 1074266112 | bytes 5767168 | tf_op jit(solution)/shard_map/dot_general | solution.py:246
  210.8 29.9 %all_to_all.46 = bf16[8,32,2048]{2,1,0:T(8,128)(2,1)S(1)} all-to-all(bf16[8,32,2048]{2,1,0:T(8,128)(2,1)S(1)} %bitcast.71), channel_id=1, replica_groups=mesh['seq'=8,'grp'=4] {'seq'}, dimensions={0} | all-to-all | bytes 2097152 | tf_op jit(solution)/shard_map/all_to_all | solution.py:247
  (59 shorter events, 8.4 us)
Async XLA Ops:
  0.0 98.0 %copy-start = (s32[256,128]{1,0:T(8,128)S(1)}, s32[256,128]{1,0:T(8,128)}, u32[]{:S(2)}) copy-start(s32[256,128]{1,0:T(8,128)} %param.17) | copy-start | bytes 393220
  16.8 6.1 %copy-start.5 = (s32[3,256]{1,0:T(4,128)S(1)}, s32[3,256]{1,0:T(4,128)}, u32[]{:S(2)}) copy-start(s32[3,256]{1,0:T(4,128)} %param.18) | copy-start | bytes 9220
  16.8 66.0 %all-to-all-start = ((f32[8,32,2560]{2,1,0:T(8,128)}), f32[8,32,2560]{2,1,0:T(8,128)S(1)}, u32[]{:S(2)}, u32[]{:S(2)}) async-start(f32[8,32,2560]{2,1,0:T(8,128)} %bitcast.68), calls=%async_computation | async-start | bytes 5242880 | tf_op jit(solution)/shard_map/all_to_all | solution.py:157
  22.8 60.1 %copy-start.4 = (f32[2560]{0:T(1024)S(1)}, f32[2560]{0:T(1024)}, u32[]{:S(2)}) copy-start(f32[2560]{0:T(1024)} %param.12) | copy-start | bytes 30724
  92.2 5.0 %copy-start.1 = (s32[256]{0:T(256)S(1)}, s32[256]{0:T(256)}, u32[]{:S(2)}) copy-start(s32[256]{0:T(256)} %param.16) | copy-start | bytes 3076
  93.5 35.3 %all-to-all-start.2 = ((bf16[8,8,80,128]{3,2,1,0:T(8,128)(2,1)}), bf16[8,8,80,128]{3,2,1,0:T(8,128)(2,1)S(1)}, u32[]{:S(2)}, u32[]{:S(2)}) async-start(bf16[8,8,80,128]{3,2,1,0:T(8,128)(2,1)} %broadcast_in_dim.174), calls=%async_computation.2 | async-start | bytes 2621440 | tf_op jit(solution)/shard_map/all_to_all | solution.py:173
  128.7 1.1 copy-start.2
  159.6 10.3 %all-to-all-start.4 = ((f32[8,1,1024]{2,1,0:T(1,128)}), f32[8,1,1024]{2,1,0:T(1,128)S(1)}, u32[]{:S(2)}, u32[]{:S(2)}) async-start(f32[8,1,1024]{2,1,0:T(1,128)} %all_to_all.38), calls=%async_computation.4 | async-start | bytes 65536 | tf_op jit(solution)/shard_map/all_to_all | solution.py:223
  169.9 28.8 %all-to-all-start.3 = ((bf16[8,64,1024]{2,1,0:T(8,128)(2,1)}), bf16[8,64,1024]{2,1,0:T(8,128)(2,1)S(1)}, u32[]{:S(2)}, u32[]{:S(2)}) async-start(bf16[8,64,1024]{2,1,0:T(8,128)(2,1)} %bitcast.64), calls=%async_computation.3 | async-start | bytes 2097152 | tf_op jit(solution)/shard_map/all_to_all | solution.py:212
  198.7 0.8 copy-start.3
where the time goes:
time: 242 us; the launch traced here: 241 us
  waiting for transfers between devices  107 us (44%)
  blocking collectives  52.5 us (22%)
  local copies, waits for them, and re-layouts  23.8 us (10%)
  Pallas kernels  20.5 us (8%)
  starting transfers between devices  17 us (7%)
  other arithmetic  11.7 us (5%)
  matrix products  8.95 us (4%)
    all_to_all x1, waiting for transfers between devices, shards(): lax.all_to_all(partial_sum.reshape(seq_count, row_share, col_count), 'seq...  58.5 us
    all_to_all x1, blocking collectives, shards(): lax.all_to_all(mixed.reshape(seq_count, row_share, mixed.shape[1]), 'seq'...  29.9 us
    all_to_all x1, waiting for transfers between devices, shards(): lax.all_to_all(jnp.broadcast_to(head_rows[None], (seq_count,) + head_rows...  28.8 us
    pallas_call x1, Pallas kernels, local_attention(): pl.pallas_call(functools.partial(attend_pages, block_pages), grid_spec=pl...  20.5 us
    all_to_all x1, waiting for transfers between devices, shards(): lax.all_to_all(local_out.astype(jnp.bfloat16).reshape(group_size, seq_cou...  16.6 us
    all_gather x1, blocking collectives, shards(): hidden_all = lax.all_gather(hidden, 'grp', axis=0, tiled=True)[send_order]  8.86 us
    slice x3, local copies, waits for them, and re-layouts, shards(): stats = jnp.stack([local_stat[:, :, 0], local_stat[:, :, HD // 2]], axis=0)  8.18 us
    all_to_all x1, blocking collectives, shards(): lax.all_to_all(outgoing, 'grp', split_axis=0, concat_axis=2, tiled=True)  7.31 us
  transfers between devices with their start and end apart: 4, of which 4 were waited for; matrix products, arithmetic and copies ran while one was open for 7% of the time, Pallas kernels for 0%

commit v1 on v0

v1 whole, which is shorter than its diff:
```python
import functools
import math

import jax
import jax.numpy as jnp
from jax import lax
from jax.experimental import pallas as pl
from jax.experimental.pallas import tpu as pltpu
from jax.sharding import PartitionSpec as P

HQ = 64
KVH = 8
HD = 128
PAGE = 128
LOW = 2
MESH = pl.DeviceIdType.MESH

rope_base = 1000000.0
neg_fill = -1e30


def greet(n_seq, n_grp):
    seq, grp = lax.axis_index("seq"), lax.axis_index("grp")
    barrier = pltpu.get_barrier_semaphore()
    for i in range(1, n_seq):
        pl.semaphore_signal(
            barrier, inc=1, device_id={"seq": lax.rem(seq + i, n_seq)}, device_id_type=MESH
        )
    for i in range(1, n_grp):
        pl.semaphore_signal(
            barrier, inc=1, device_id={"grp": lax.rem(grp + i, n_grp)}, device_id_type=MESH
        )
    pl.semaphore_wait(barrier, n_seq + n_grp - 2)


def send(src, dst, send_sem, recv_sem, axis, index):
    copy = pltpu.make_async_remote_copy(
        src_ref=src,
        dst_ref=dst,
        send_sem=send_sem,
        recv_sem=recv_sem,
        device_id={axis: index},
        device_id_type=MESH,
    )
    copy.start()
    return copy


def arrived(ref, sem):
    pltpu.make_async_copy(ref, ref, sem).wait()


def gather_groups(n_grp, own_ref, all_ref, send_sem, recv_sem):
    grp = lax.axis_index("grp")
    high_count = n_grp // LOW
    high, low = grp // LOW, lax.rem(grp, LOW)
    copies = [
        send(own_ref, all_ref.at[grp], send_sem.at[i - 1], recv_sem.at[grp], "grp",
             lax.rem(high + i, high_count) * LOW + low)
        for i in range(1, high_count)
    ]
    other = grp + 1 - 2 * low
    copies.append(
        send(own_ref, all_ref.at[grp], send_sem.at[high_count - 1], recv_sem.at[grp], "grp", other)
    )
    all_ref[grp] = own_ref[...]
    for i in range(1, high_count):
        block = lax.rem(high + high_count - i, high_count) * LOW + low
        arrived(all_ref.at[block], recv_sem.at[block])
        copies.append(
            send(all_ref.at[block], all_ref.at[block], send_sem.at[high_count - 1 + i],
                 recv_sem.at[block], "grp", other)
        )
    for h in range(high_count):
        block = h * LOW + 1 - low
        arrived(all_ref.at[block], recv_sem.at[block])
    return copies


def project_kernel(n_seq, n_grp, hidden_ref, perm_ref, w_hbm, bias_ref, cos_ref, sin_ref,
                   q_ref, nv_ref, hid_all, rows_ref, w_ref, own_ref, y_send, y_recv, z_send,
                   z_recv, turned_ref, d_send, d_recv, x_ref, wide_ref, block_ref, nv_send,
                   w_sem, g_send, g_recv, ys_sem, yr_sem, zs_sem, zr_sem, ds_sem, dr_sem,
                   qs_sem, qr_sem, ns_sem, nr_sem):
    pieces, depth, width = w_ref.shape
    seq, grp = lax.axis_index("seq"), lax.axis_index("grp")
    high_count = n_seq // LOW
    high, low = seq // LOW, lax.rem(seq, LOW)
    pair = seq + 1 - 2 * low
    half = rows_ref.shape[0] // LOW
    row_share = half // high_count
    share = row_share // n_grp
    piece_heads = width // HD
    block_heads = pieces * piece_heads
    head_share = HQ // n_seq
    group_q = HQ // KVH

    def fetch(p):
        return pltpu.make_async_copy(
            w_hbm.at[:, pl.ds(pl.multiple_of(p * width, width), width)], w_ref.at[p], w_sem.at[p]
        )

    for p in range(pieces):
        fetch(p).start()
    greet(n_seq, n_grp)
    hidden_sends = gather_groups(n_grp, hidden_ref, hid_all, g_send, g_recv)
    rows_ref[...] = jnp.dot(
        perm_ref[...], hid_all[...].reshape(-1, depth), preferred_element_type=jnp.float32
    ).astype(jnp.bfloat16)

    def y_copy(p):
        return pltpu.make_async_remote_copy(
            src_ref=y_send.at[p], dst_ref=y_recv.at[p], send_sem=ys_sem.at[p],
            recv_sem=yr_sem.at[p], device_id={"seq": pair}, device_id_type=MESH)

    def multiply(p, carry):
        fetch(p).wait()
        theirs = rows_ref[pl.ds(pl.multiple_of((1 - low) * half, half), half), :]
        y_send[p] = jnp.dot(theirs, w_ref[p], preferred_element_type=jnp.float32)
        y_copy(p).start()
        mine = rows_ref[pl.ds(pl.multiple_of(low * half, half), half), :]
        own_ref[p] = jnp.dot(mine, w_ref[p], preferred_element_type=jnp.float32)
        return carry

    lax.fori_loop(0, pieces, multiply, 0)

    def z_copy(p, i):
        peer = lax.rem(high + i, high_count)
        return pltpu.make_async_remote_copy(
            src_ref=z_send.at[p, peer], dst_ref=z_recv.at[p, i - 1], send_sem=zs_sem.at[p, i - 1],
            recv_sem=zr_sem.at[p, i - 1], device_id={"seq": peer * LOW + low},
            device_id_type=MESH)

    def spread(p):
        y_copy(p).wait_recv()
        z_send[p] = (own_ref[p] + y_recv[p]).reshape(high_count, row_share, width)
        for i in range(1, high_count):
            z_copy(p, i).start()

    def finish(p):
        total = z_send[p, high]
        for i in range(1, high_count):
            z_copy(p, i).wait_recv()
            total = total + z_recv[p, i - 1]
        total = total + bias_ref[p]
        for k in range(piece_heads):
            values = total[:, k * HD : (k + 1) * HD]
            rotated = values * cos_ref[...] + pltpu.roll(values, HD // 2, 1) * sin_ref[...]
            head = p * piece_heads + k
            values = jnp.where(grp * block_heads + head < HQ + KVH, rotated, values)
            for g in range(n_grp):
                turned_ref[g, pl.ds(head, share, stride=block_heads), :] = values[
                    g * share : (g + 1) * share
                ]

    spread(0)

    def step(p, carry):
        spread(p)
        finish(p - 1)
        return carry

    lax.fori_loop(1, pieces, step, 0)
    finish(pieces - 1)

    d_send[...] = turned_ref[...].astype(jnp.bfloat16)
    head_sends = []
    for i in range(1, n_grp):
        peer = lax.rem(grp + i, n_grp)
        head_sends.append(
            send(d_send.at[peer], d_recv.at[i - 1], ds_sem.at[i - 1], dr_sem.at[i - 1], "grp", peer)
        )
    x_ref[grp] = d_send[grp].astype(jnp.float32)
    for i in range(1, n_grp):
        head_sends[i - 1].wait_recv()
        x_ref[lax.rem(grp + n_grp - i, n_grp)] = d_recv[i - 1].astype(jnp.float32)

    def head_rows(head):
        return x_ref[head // block_heads, pl.ds(head % block_heads, share, stride=block_heads), :]

    for head in range(HQ):
        wide_ref[pl.ds(head, share, stride=HQ), :] = head_rows(head)
    block_ref[...] = wide_ref[...].reshape(share, HQ, HD).astype(jnp.bfloat16)

    def rows_of(index):
        return q_ref.at[pl.ds(index * share, share)]

    q_sends = []
    for i in range(1, high_count):
        peer = lax.rem(high + i, high_count) * LOW + low
        q_sends.append(
            send(block_ref, rows_of(seq), qs_sem.at[i - 1], qr_sem.at[seq], "seq", peer)
        )
    q_sends.append(
        send(block_ref, rows_of(seq), qs_sem.at[high_count - 1], qr_sem.at[seq], "seq", pair)
    )
    q_ref[pl.ds(seq * share, share)] = block_ref[...]

    lane = lax.broadcasted_iota(jnp.int32, (share, HD), 1)
    for peer in range(n_seq):
        kv = peer * head_share // group_q
        scores = jnp.zeros((share, HD), jnp.float32)
        for k in range(head_share):
            head = peer * head_share + k
            key = head_rows(HQ + head // group_q)
            score = jnp.sum(head_rows(head) * key, axis=1, keepdims=True) * (HD**-0.5)
            scores = jnp.where(lane == k, score, scores)
        nv_send[peer, 0] = scores
        nv_send[peer, 1] = head_rows(HQ + KVH + kv)
    nv_sends = []
    for i in range(1, n_seq):
        peer = lax.rem(seq + i, n_seq)
        nv_sends.append(
            send(nv_send.at[peer], nv_ref.at[seq], ns_sem.at[i - 1], nr_sem.at[seq], "seq", peer)
        )
    nv_ref[seq] = nv_send[seq]

    for i in range(1, high_count):
        block = lax.rem(high + high_count - i, high_count) * LOW + low
        arrived(rows_of(block), qr_sem.at[block])
        q_sends.append(
            send(rows_of(block), rows_of(block), qs_sem.at[high_count - 1 + i], qr_sem.at[block],
                 "seq", pair)
        )
    for h in range(high_count):
        block = h * LOW + 1 - low
        arrived(rows_of(block), qr_sem.at[block])
    for i in range(1, n_seq):
        block = lax.rem(seq + i, n_seq)
        arrived(nv_ref.at[block], nr_sem.at[block])

    def drain(p, carry):
        y_copy(p).wait_send()
        for i in range(1, high_count):
            z_copy(p, i).wait_send()
        return carry

    lax.fori_loop(0, pieces, drain, 0)
    for copy in hidden_sends + head_sends + q_sends + nv_sends:
        copy.wait_send()


def project(n_seq, n_grp, hidden, perm, w_qkv, bias, cosine, sine):
    group_size, depth = hidden.shape
    request_total = perm.shape[0]
    col_count = w_qkv.shape[1]
    pieces = math.gcd(col_count // HD, 5)
    width = col_count // pieces
    half = request_total // LOW
    high_count = n_seq // LOW
    row_share = half // high_count
    share = row_share // n_grp
    block_rows = share * col_count // HD
    dma = pltpu.SemaphoreType.DMA
    vmem = pl.BlockSpec(memory_space=pltpu.VMEM)
    return pl.pallas_call(
        functools.partial(project_kernel, n_seq, n_grp),
        out_shape=[
            jax.ShapeDtypeStruct((group_size, HQ, HD), jnp.bfloat16),
            jax.ShapeDtypeStruct((n_seq, 2, share, HD), jnp.float32),
        ],
        in_specs=[vmem, vmem, pl.BlockSpec(memory_space=pl.ANY), vmem, vmem, vmem],
        out_specs=[vmem, vmem],
        scratch_shapes=[
            pltpu.VMEM((n_grp, group_size, depth), jnp.bfloat16),
            pltpu.VMEM((request_total, depth), jnp.bfloat16),
            pltpu.VMEM((pieces, depth, width), jnp.bfloat16),
            pltpu.VMEM((pieces, half, width), jnp.float32),
            pltpu.VMEM((pieces, half, width), jnp.float32),
            pltpu.VMEM((pieces, half, width), jnp.float32),
            pltpu.VMEM((pieces, high_count, row_share, width), jnp.float32),
            pltpu.VMEM((pieces, high_count - 1, row_share, width), jnp.float32),
            pltpu.VMEM((n_grp, block_rows, HD), jnp.float32),
            pltpu.VMEM((n_grp, block_rows, HD), jnp.bfloat16),
            pltpu.VMEM((n_grp - 1, block_rows, HD), jnp.bfloat16),
            pltpu.VMEM((n_grp, block_rows, HD), jnp.float32),
            pltpu.VMEM((share * HQ, HD), jnp.float32),
            pltpu.VMEM((share, HQ, HD), jnp.bfloat16),
            pltpu.VMEM((n_seq, 2, share, HD), jnp.float32),
            dma((pieces,)),
            dma((2 * n_grp,)),
            dma((n_grp,)),
            dma((pieces,)),
            dma((pieces,)),
            dma((pieces, high_count - 1)),
            dma((pieces, high_count - 1)),
            dma((n_grp - 1,)),
            dma((n_grp - 1,)),
            dma((2 * high_count,)),
            dma((n_seq,)),
            dma((n_seq - 1,)),
            dma((n_seq,)),
        ],
        compiler_params=pltpu.CompilerParams(
            collective_id=0, has_side_effects=True, vmem_limit_bytes=56 * 1024 * 1024
        ),
        cost_estimate=pl.CostEstimate(
            flops=2 * request_total * depth * col_count,
            bytes_accessed=2 * depth * col_count,
            transcendentals=0,
        ),
    )(hidden, perm, w_qkv, bias.reshape(pieces, 1, width), cosine, sine)


def attend_pages(block_pages, owner_ref, live_ref, rows_ref, key_ref, value_ref, out_ref, stat_ref,
                 wide_ref):
    step = pl.program_id(0)
    group_q = HQ // KVH
    width = KVH * HD
    pool_pages = out_ref.shape[1]

    @pl.when(step == 0)
    def _():
        stat_ref[...] = jnp.zeros_like(stat_ref)

    row_head = lax.broadcasted_iota(jnp.int32, (HQ, width), 0) // group_q
    col_head = lax.broadcasted_iota(jnp.int32, (HQ, width), 1) // HD
    own_head = (row_head == col_head).astype(jnp.float32).astype(jnp.bfloat16)
    place = lax.broadcasted_iota(jnp.int32, (HQ, PAGE), 1)
    lane = lax.broadcasted_iota(jnp.int32, (HQ, HD), 1)
    stat = stat_ref[...].reshape(HQ, HD)
    for j in range(block_pages):
        page = step * block_pages + j
        owner = owner_ref[page]
        alive = place < live_ref[page]
        query = rows_ref[owner]
        spread = jnp.concatenate([query] * KVH, axis=1) * own_head
        keys = key_ref[0, j * PAGE : (j + 1) * PAGE, :]
        values = value_ref[0, j * PAGE : (j + 1) * PAGE, :]
        scores = lax.dot_general(
            spread, keys, (((1,), (1,)), ((), ())), preferred_element_type=jnp.float32
        ) * (HD**-0.5)
        scores = jnp.where(alive, scores, neg_fill)
        page_max = jnp.max(scores, axis=1, keepdims=True)
        weights = jnp.where(alive, jnp.exp(scores - page_max), 0.0)
        page_total = jnp.sum(weights, axis=1, keepdims=True)
        wide = jnp.dot(weights.astype(jnp.bfloat16), values, preferred_element_type=jnp.float32)
        page_out = jnp.concatenate(
            [
                wide[h * group_q : (h + 1) * group_q, h * HD : (h + 1) * HD]
                for h in range(KVH)
            ],
            axis=0,
        )
        wide_ref[pl.ds(page, HQ, stride=pool_pages), :] = page_out
        holder = jnp.where(live_ref[page] > 0, owner, -1).astype(jnp.float32)
        stat = jnp.where(lane == page, page_max, stat)
        stat = jnp.where(lane == pool_pages + page, page_total, stat)
        stat = jnp.where(lane == 2 * pool_pages + page, holder, stat)
    stat_ref[...] = stat.reshape(stat_ref.shape)

    @pl.when(step == pl.num_programs(0) - 1)
    def _():
        out_ref[...] = wide_ref[...].reshape(out_ref.shape).astype(jnp.bfloat16)


def local_attention(n_seq, owner, live, rows, k_cache, v_cache):
    group_size = rows.shape[0]
    pool_pages = k_cache.shape[1] // PAGE
    block_pages = math.gcd(pool_pages, 4)
    cache_spec = pl.BlockSpec((1, block_pages * PAGE, KVH * HD), lambda i, *_: (0, i, 0))
    out_shape = [
        jax.ShapeDtypeStruct((HQ, pool_pages, HD), jnp.bfloat16),
        jax.ShapeDtypeStruct((n_seq, HQ // n_seq, HD), jnp.float32),
    ]
    return pl.pallas_call(
        functools.partial(attend_pages, block_pages),
        grid_spec=pltpu.PrefetchScalarGridSpec(
            num_scalar_prefetch=2,
            grid=(pool_pages // block_pages,),
            in_specs=[
                pl.BlockSpec(rows.shape, lambda i, *_: (0, 0, 0)),
                cache_spec,
                cache_spec,
            ],
            out_specs=[
                pl.BlockSpec(shape.shape, lambda i, *_: (0, 0, 0)) for shape in out_shape
            ],
            scratch_shapes=[pltpu.VMEM((HQ * pool_pages, HD), jnp.float32)],
        ),
        out_shape=out_shape,
        compiler_params=pltpu.CompilerParams(
            dimension_semantics=("arbitrary",), vmem_limit_bytes=56 * 1024 * 1024
        ),
        cost_estimate=pl.CostEstimate(
            flops=4 * pool_pages * HQ * PAGE * KVH * HD,
            bytes_accessed=4 * pool_pages * PAGE * KVH * HD,
            transcendentals=pool_pages * HQ * PAGE,
        ),
    )(owner, live, rows, k_cache, v_cache)


def mix_kernel(n_seq, n_grp, out_ref, stat_ref, nv_ref, perm_ref, w_hbm, mixed_ref,
               o_all, s_all, att_ref, att_all, rows_ref, w_ref, own_ref, y_send, y_recv, z_keep,
               z_send, z_recv, w_sem, os_sem, or_sem, ss_sem, sr_sem, g_send, g_recv,
               ys_sem, yr_sem, zs_sem, zr_sem):
    pieces, depth, width = w_ref.shape
    seq = lax.axis_index("seq")
    high_count = n_seq // LOW
    high, low = seq // LOW, lax.rem(seq, LOW)
    pair = seq + 1 - 2 * low
    half = rows_ref.shape[0] // LOW
    row_share = half // high_count
    head_share = HQ // n_seq
    pool_pages = out_ref.shape[1]
    slots = n_seq * pool_pages
    packed = HD // pool_pages
    group_size = att_ref.shape[0]

    def fetch(p):
        return pltpu.make_async_copy(
            w_hbm.at[:, pl.ds(pl.multiple_of(p * width, width), width)], w_ref.at[p], w_sem.at[p]
        )

    for p in range(pieces):
        fetch(p).start()
    greet(n_seq, n_grp)
    slot_sends = []
    for i in range(1, n_seq):
        peer = lax.rem(seq + i, n_seq)
        slot_sends.append(
            send(stat_ref.at[peer], s_all.at[seq], ss_sem.at[i - 1], sr_sem.at[seq], "seq", peer)
        )
        slot_sends.append(
            send(out_ref.at[pl.ds(peer * head_share, head_share)], o_all.at[seq], os_sem.at[i - 1],
                 or_sem.at[seq], "seq", peer)
        )
    s_all[seq] = stat_ref[seq]
    o_all[seq] = out_ref[pl.ds(seq * head_share, head_share)]
    for i in range(1, n_seq):
        peer = lax.rem(seq + i, n_seq)
        arrived(s_all.at[peer], sr_sem.at[peer])

    spot = lax.broadcasted_iota(jnp.int32, (head_share, HD), 1) // pool_pages

    def lined_up(field):
        tiles = []
        for first in range(0, n_seq, packed):
            tile = jnp.zeros((head_share, HD), jnp.float32)
            for k in range(packed):
                shift = (HD + (k - field) * pool_pages) % HD
                source = s_all[first + k]
                tile = jnp.where(spot == k, pltpu.roll(source, shift, 1) if shift else source, tile)
            tiles.append(tile)
        return jnp.concatenate(tiles, axis=1)

    tops, totals, holders = lined_up(0), lined_up(1), lined_up(2)
    request = lax.broadcasted_iota(jnp.int32, (group_size, slots), 0).astype(jnp.float32)
    held = request == holders[:1, :]
    fresh_scores = nv_ref[:, 0].reshape(group_size, HD)
    fresh_values = nv_ref[:, 1].reshape(group_size, HD)
    for i in range(1, n_seq):
        peer = lax.rem(seq + i, n_seq)
        arrived(o_all.at[peer], or_sem.at[peer])
    for k in range(head_share):
        top = jnp.where(held, tops[k : k + 1, :], neg_fill)
        fresh = fresh_scores[:, k : k + 1]
        peak = jnp.maximum(jnp.max(top, axis=1, keepdims=True), fresh)
        factor = jnp.where(held, jnp.exp(top - peak), 0.0)
        fresh_weight = jnp.exp(fresh - peak)
        denominator = jnp.sum(factor * totals[k : k + 1, :], axis=1, keepdims=True) + fresh_weight
        coarse = factor.astype(jnp.bfloat16)
        fine = (factor - coarse.astype(jnp.float32)).astype(jnp.bfloat16)
        outs = o_all[:, k].reshape(slots, HD)
        numerator = (
            jnp.dot(coarse, outs, preferred_element_type=jnp.float32)
            + jnp.dot(fine, outs, preferred_element_type=jnp.float32)
            + fresh_weight * fresh_values
        )
        att_ref[:, k * HD : (k + 1) * HD] = (numerator / denominator).astype(jnp.bfloat16)

    att_sends = gather_groups(n_grp, att_ref, att_all, g_send, g_recv)
    rows_ref[...] = jnp.dot(
        perm_ref[...], att_all[...].reshape(-1, depth), preferred_element_type=jnp.float32
    ).astype(jnp.bfloat16)

    def y_copy(p):
        return pltpu.make_async_remote_copy(
            src_ref=y_send.at[p], dst_ref=y_recv.at[p], send_sem=ys_sem.at[p],
            recv_sem=yr_sem.at[p], device_id={"seq": pair}, device_id_type=MESH)

    def multiply(p, carry):
        fetch(p).wait()
        theirs = rows_ref[pl.ds(pl.multiple_of((1 - low) * half, half), half), :]
        y_send[p] = jnp.dot(theirs, w_ref[p], preferred_element_type=jnp.float32).astype(
            jnp.bfloat16
        )
        y_copy(p).start()
        mine = rows_ref[pl.ds(pl.multiple_of(low * half, half), half), :]
        own_ref[p] = jnp.dot(mine, w_ref[p], preferred_element_type=jnp.float32)
        return carry

    lax.fori_loop(0, pieces, multiply, 0)

    def z_copy(p, i):
        peer = lax.rem(high + i, high_count)
        return pltpu.make_async_remote_copy(
            src_ref=z_send.at[p, peer], dst_ref=z_recv.at[p, i - 1], send_sem=zs_sem.at[p, i - 1],
            recv_sem=zr_sem.at[p, i - 1], device_id={"seq": peer * LOW + low},
            device_id_type=MESH)

    def spread(p, carry):
        y_copy(p).wait_recv()
        z_keep[p] = (own_ref[p] + y_recv[p].astype(jnp.float32)).reshape(
            high_count, row_share, width
        )
        z_send[p] = z_keep[p].astype(jnp.bfloat16)
        for i in range(1, high_count):
            z_copy(p, i).start()
        return carry

    lax.fori_loop(0, pieces, spread, 0)
    for p in range(pieces):
        total = z_keep[p, high]
        for i in range(1, high_count):
            z_copy(p, i).wait_recv()
            total = total + z_recv[p, i - 1].astype(jnp.float32)
        mixed_ref[:, p * width : (p + 1) * width] = total.astype(jnp.bfloat16)

    def drain(p, carry):
        y_copy(p).wait_send()
        for i in range(1, high_count):
            z_copy(p, i).wait_send()
        return carry

    lax.fori_loop(0, pieces, drain, 0)
    for copy in slot_sends + att_sends:
        copy.wait_send()


def mix(n_seq, n_grp, outs, stats, nv, perm, w_out):
    request_total = perm.shape[0]
    group_size = request_total // n_grp
    depth, col_count = w_out.shape
    pieces = math.gcd(col_count // HD, 4)
    width = col_count // pieces
    half = request_total // LOW
    high_count = n_seq // LOW
    row_share = half // high_count
    head_share = HQ // n_seq
    pool_pages = outs.shape[1]
    dma = pltpu.SemaphoreType.DMA
    vmem = pl.BlockSpec(memory_space=pltpu.VMEM)
    return pl.pallas_call(
        functools.partial(mix_kernel, n_seq, n_grp),
        out_shape=jax.ShapeDtypeStruct((row_share, col_count), jnp.bfloat16),
        in_specs=[vmem, vmem, vmem, vmem, pl.BlockSpec(memory_space=pl.ANY)],
        out_specs=vmem,
        scratch_shapes=[
            pltpu.VMEM((n_seq, head_share, pool_pages, HD), jnp.bfloat16),
            pltpu.VMEM((n_seq, head_share, HD), jnp.float32),
            pltpu.VMEM((group_size, depth), jnp.bfloat16),
            pltpu.VMEM((n_grp, group_size, depth), jnp.bfloat16),
            pltpu.VMEM((request_total, depth), jnp.bfloat16),
            pltpu.VMEM((pieces, depth, width), jnp.bfloat16),
            pltpu.VMEM((pieces, half, width), jnp.float32),
            pltpu.VMEM((pieces, half, width), jnp.bfloat16),
            pltpu.VMEM((pieces, half, width), jnp.bfloat16),
            pltpu.VMEM((pieces, high_count, row_share, width), jnp.float32),
            pltpu.VMEM((pieces, high_count, row_share, width), jnp.bfloat16),
            pltpu.VMEM((pieces, high_count - 1, row_share, width), jnp.bfloat16),
            dma((pieces,)),
            dma((n_seq - 1,)),
            dma((n_seq,)),
            dma((n_seq - 1,)),
            dma((n_seq,)),
            dma((2 * n_grp,)),
            dma((n_grp,)),
            dma((pieces,)),
            dma((pieces,)),
            dma((pieces, high_count - 1)),
            dma((pieces, high_count - 1)),
        ],
        compiler_params=pltpu.CompilerParams(
            collective_id=1, has_side_effects=True, vmem_limit_bytes=56 * 1024 * 1024
        ),
        cost_estimate=pl.CostEstimate(
            flops=2 * request_total * depth * col_count,
            bytes_accessed=2 * depth * col_count,
            transcendentals=0,
        ),
    )(outs, stats, nv, perm, w_out)


def rope_tables(places):
    freq_index = jnp.arange(HD // 2, dtype=jnp.int32)
    inverse_freq = jnp.exp(freq_index.astype(jnp.float32) * (-2.0 * math.log(rope_base) / HD))
    section = jnp.where(
        freq_index < HD // 8, 0, jnp.where(freq_index < HD // 8 + 3 * HD // 16, 1, 2)
    )
    place_float = places.astype(jnp.float32)
    chosen = jnp.where(
        section[None, :] == 0,
        place_float[0][:, None],
        jnp.where(section[None, :] == 1, place_float[1][:, None], place_float[2][:, None]),
    )
    angles = chosen * inverse_freq[None, :]
    cosine, sine = jnp.cos(angles), jnp.sin(angles)
    return jnp.concatenate([cosine, cosine], 1), jnp.concatenate([-sine, sine], 1)


def shards(hidden, w_qkv, b_qkv, w_out, k_cache, v_cache, lengths, page_table, positions, group_of):
    n_seq = lax.axis_size("seq")
    n_grp = lax.axis_size("grp")
    seq_index = lax.axis_index("seq")
    grp_index = lax.axis_index("grp")
    request_total = group_of.shape[0]
    group_size = request_total // n_grp
    share = group_size // n_seq
    high_count = n_seq // LOW
    row_share = request_total // n_seq
    request_ids = jnp.arange(request_total, dtype=jnp.int32)
    before = (group_of[None, :] < group_of[:, None]) | (group_of[None, :] == group_of[:, None]) & (
        request_ids[None, :] < request_ids[:, None]
    )
    served_at = jnp.sum(before.astype(jnp.int32), axis=1)
    rank = served_at % group_size
    holder = rank // share
    sent_at = (
        ((holder % LOW) * high_count + holder // LOW) * n_grp + served_at // group_size
    ) * share + rank % share
    in_perm = sent_at[None, :] == request_ids[:, None]
    my_start = ((seq_index % LOW) * high_count + seq_index // LOW) * row_share
    my_rows = (
        my_start + jnp.arange(row_share, dtype=jnp.int32)[:, None] == sent_at[None, :]
    )
    places = jnp.sum(jnp.where(my_rows[None], positions[:, None, :], 0), axis=2)
    cosine, sine = rope_tables(places)
    rows, nv = project(
        n_seq, n_grp, hidden, in_perm.astype(jnp.bfloat16), w_qkv, b_qkv, cosine, sine
    )

    placed_at = served_at[None, :] == request_ids[:, None]
    served_order = jnp.sum(jnp.where(placed_at, request_ids[None, :], 0), axis=1)
    served_ids = lax.dynamic_slice_in_dim(served_order, grp_index * group_size, group_size, 0)
    served_len = lengths[served_ids]
    served_table = page_table[served_ids]
    most_pages = page_table.shape[1]
    page_counts = (served_len + PAGE - 1) // PAGE
    logical = jnp.arange(most_pages, dtype=jnp.int32)
    pool_pages = k_cache.shape[1] // PAGE
    local_page = served_table - seq_index * pool_pages
    usable = (
        (logical[None, :] < page_counts[:, None]) & (local_page >= 0) & (local_page < pool_pages)
    )
    pool_ids = jnp.arange(pool_pages, dtype=jnp.int32)
    matched = usable[:, :, None] & (local_page[:, :, None] == pool_ids[None, None, :])
    owner_ids = jnp.arange(group_size, dtype=jnp.int32)
    left = served_len[:, None] - logical[None, :] * PAGE
    live = jnp.max(jnp.where(matched, left[:, :, None], 0), axis=(0, 1))
    owner = jnp.max(jnp.where(matched, owner_ids[:, None, None], 0), axis=(0, 1))
    outs, stats = local_attention(n_seq, owner, live, rows, k_cache, v_cache)

    back_at = served_at.reshape(high_count, LOW, row_share).transpose(1, 0, 2).reshape(-1)
    out_perm = back_at[:, None] == request_ids[None, :]
    return mix(n_seq, n_grp, outs, stats, nv, out_perm.astype(jnp.bfloat16), w_out)


def solution(mesh):
    placed = (
        P("grp", "seq"),
        P("seq", "grp"),
        P("grp"),
        P("seq", "grp"),
        P("grp", "seq", None),
        P("grp", "seq", None),
        P(),
        P(),
        P(),
        P(),
    )
    return jax.shard_map(
        shards, mesh=mesh, in_specs=placed, out_specs=P("seq", "grp"), check_vma=False
    )
```

time: 242 us -> 146 us (0.60)
  Pallas kernels: 20.5 us -> 135 us
  waiting for transfers between devices: 107 us -> 0 us
  blocking collectives: 52.5 us -> 0 us
  local copies, waits for them, and re-layouts: 23.8 us -> 5.14 us
  starting transfers between devices: 17 us -> 0 us
  matrix products: 8.95 us -> 0 us
  other arithmetic: 11.7 us -> 5.72 us
    pallas_call x0 -> x2, Pallas kernels: none -> 118 us  [the longest x1 71.8 us: project(): pl.pallas_call(functools.partial(project_kernel, n_seq, n_grp), out_shape...]
    all_to_all x4 -> x0, waiting for transfers between devices: 107 us -> none  [the longest x1 58.5 us: shards(): lax.all_to_all(partial_sum.reshape(seq_count, row_share, col_count), 'seq...]
    all_to_all x2 -> x0, blocking collectives: 37.2 us -> none  [the longest x1 29.9 us: shards(): lax.all_to_all(mixed.reshape(seq_count, row_share, mixed.shape[1]), 'seq'...]
    all_to_all x4 -> x0, starting transfers between devices: 17 us -> none  [the longest x1 5.97 us: shards(): lax.all_to_all(partial_sum.reshape(seq_count, row_share, col_count), 'seq...]
    all_gather x2 -> x0, blocking collectives: 15.4 us -> none  [the longest x1 8.86 us: shards(): hidden_all = lax.all_gather(hidden, 'grp', axis=0, tiled=True)[send_order]]
    dot_general x2 -> x0, matrix products: 8.95 us -> none  [the longest x1 5.51 us: shards(): partial_sum = jnp.dot(hidden_all, w_qkv, preferred_element_type=jnp.float32)]
    slice x4 -> x0, local copies, waits for them, and re-layouts: 8.35 us -> none  [the longest x3 8.18 us: shards(): stats = jnp.stack([local_stat[:, :, 0], local_stat[:, :, HD // 2]], axis=0)]
    convert_element_type x5 -> x3, other arithmetic: 5.09 us -> 1.45 us  [the longest x1 0.76 us: shards(): out_perm.astype(jnp.bfloat16)]
  transfers between devices with their start and end apart: 4 -> 0, of which waited for: 4 -> 0; matrix products, arithmetic and copies ran while one was open for 7% -> 0% of each run, Pallas kernels for 0% -> 0%
where the time goes in v1:
time: 146 us
  Pallas kernels  135 us (92%)
  other arithmetic  5.72 us (4%)
  local copies, waits for them, and re-layouts  5.14 us (4%)
    pallas_call x1, Pallas kernels, project(): pl.pallas_call(functools.partial(project_kernel, n_seq, n_grp), out_shape...  71.8 us
    pallas_call x1, Pallas kernels, mix(): pl.pallas_call(functools.partial(mix_kernel, n_seq, n_grp), out_shape=jax...  45.9 us
    pallas_call x1, Pallas kernels, local_attention(): pl.pallas_call(functools.partial(attend_pages, block_pages), grid_spec=pl...  17.5 us

profile of v1, /device:TPU:0, one launch (start us, length us, event | category | flops | bytes accessed | tf_op | source)
XLA Modules:
  0.0 146.1 jit_solution(14029236325416858523)
XLA Ops:
  0.0 0.0 copy-start
  0.0 0.9 convert_reduce_fusion
  1.0 0.1 broadcast_compare_fusion
  1.1 0.8 select_reduce_fusion.3
  2.0 0.2 fusion.13
  2.1 0.7 pad_maximum_fusion
  2.8 0.7 fusion.3.perm_ref
  3.5 1.3 reshape.232.bias_ref
  4.8 71.8 %shard_map.100 = (bf16[64,64,128]{2,1,0:T(8,128)(2,1)}, f32[8,2,8,128]{3,2,1,0:T(8,128)}) custom-call(bf16[64,1024]{1,0:T(8,128)(2,1)} %hidden_ref.1, bf16[256,256]{1,0:T(8,128)(2,1)} %fusion.3.perm_ref, bf16[1024,2560]{1,0:T(8,128)(2,1)} %w_hbm.2, f32[5,1,512]{2,1,0:T(1,128)} %reshape.232.bias_ref, f32[32,128]{1,0:T(8,128)} %get-tuple-element.23.cos_ref, ...), custom_call_target="tpu_custom_call" | custom-call | flops 1342177280 | bytes 5242880 | tf_op jit(solution)/shard_map/pallas_call | solution.py:256
  76.7 0.1 select_reduce_fusion.2
  76.8 0.1 compare_select_fusion
  76.9 1.5 %gather_fusion = s32[64]{0:T(128)S(1)} fusion(s32[256]{0:T(256)} %param.16, s32[1024]{0:T(1024)S(1)} %pad_clamp_fusion), kind=kCustom, calls=%fused_computation | custom fusion | bytes 768 | tf_op jit(solution)/shard_map/gather | solution.py:636
  78.4 0.0 copy-done
  78.4 0.6 gather_fusion.1
  79.0 0.1 fusion.6
  79.0 0.1 broadcast_subtract_fusion
  79.1 1.1 select_reduce_fusion
  80.3 17.5 %shard_map.101 = (bf16[64,32,128]{2,1,0:T(8,128)(2,1)}, f32[8,8,128]{2,1,0:T(8,128)}) custom-call(s32[32]{0:T(128)} %get-tuple-element.14.owner_ref, s32[32]{0:T(128)} %get-tuple-element.13.live_ref, bf16[64,64,128]{2,1,0:T(8,128)(2,1)} %get-tuple-element.9.rows_ref, bf16[1,4096,1024]{2,1,0:T(8,128)(2,1)} %key_ref.1, bf16[1,4096,1024]{2,1,0:T(8,128)(2,1)} %value_ref.1), custom_call_target="tpu_custom_call" | custom-call | flops 1073741824 | bytes 16777216 | tf_op jit(solution)/shard_map/pallas_call | solution.py:366
  97.8 0.1 reshape.233
  97.9 0.1 eq.111
  97.9 0.8 fusion.4.perm_ref
  98.7 45.9 %shard_map.102 = bf16[32,2048]{1,0:T(8,128)(2,1)} custom-call(bf16[64,32,128]{2,1,0:T(8,128)(2,1)} %get-tuple-element.10.out_ref, f32[8,8,128]{2,1,0:T(8,128)} %get-tuple-element.11.stat_ref, f32[8,2,8,128]{3,2,1,0:T(8,128)} %get-tuple-element.12.nv_ref, bf16[256,256]{1,0:T(8,128)(2,1)} %fusion.4.perm_ref, bf16[1024,2048]{1,0:T(8,128)(2,1)} %w_hbm.3), custom_call_target="tpu_custom_call" | custom-call | flops 1073741824 | bytes 4194304 | tf_op jit(solution)/shard_map/pallas_call | solution.py:544
  144.6 1.6 %copy.14 = bf16[32,2048]{1,0:T(8,128)(2,1)} copy(bf16[32,2048]{1,0:T(8,128)(2,1)} %shard_map.102) | data formatting | bytes 262144
  (11 shorter events, 0.1 us)
Async XLA Ops:
  0.0 78.4 %copy-start = (s32[256,128]{1,0:T(8,128)S(1)}, s32[256,128]{1,0:T(8,128)}, u32[]{:S(2)}) copy-start(s32[256,128]{1,0:T(8,128)} %param.17) | copy-start | bytes 393220

commit v2 on v0

v2 whole, which is shorter than its diff:
```python
import functools
import math

import jax
import jax.numpy as jnp
from jax import lax
from jax.experimental import pallas as pl
from jax.experimental.pallas import tpu as pltpu
from jax.sharding import PartitionSpec as P

HQ = 64
KVH = 8
HD = 128
PAGE = 128
LOW = 2
MESH = pl.DeviceIdType.MESH

rope_base = 1000000.0
neg_fill = -1e30


def greet(n_seq, n_grp):
    seq, grp = lax.axis_index("seq"), lax.axis_index("grp")
    barrier = pltpu.get_barrier_semaphore()
    for i in range(1, n_seq):
        pl.semaphore_signal(
            barrier, inc=1, device_id={"seq": lax.rem(seq + i, n_seq)}, device_id_type=MESH
        )
    for i in range(1, n_grp):
        pl.semaphore_signal(
            barrier, inc=1, device_id={"grp": lax.rem(grp + i, n_grp)}, device_id_type=MESH
        )
    pl.semaphore_wait(barrier, n_seq + n_grp - 2)


def send(src, dst, send_sem, recv_sem, axis, index):
    copy = pltpu.make_async_remote_copy(
        src_ref=src,
        dst_ref=dst,
        send_sem=send_sem,
        recv_sem=recv_sem,
        device_id={axis: index},
        device_id_type=MESH,
    )
    copy.start()
    return copy


def arrived(ref, sem):
    pltpu.make_async_copy(ref, ref, sem).wait()


def gather_start(n_grp, own_ref, all_ref, send_sem, recv_sem):
    grp = lax.axis_index("grp")
    high_count = n_grp // LOW
    high, low = grp // LOW, lax.rem(grp, LOW)
    copies = [
        send(own_ref, all_ref.at[grp], send_sem.at[i - 1], recv_sem.at[grp], "grp",
             lax.rem(high + i, high_count) * LOW + low)
        for i in range(1, high_count)
    ]
    copies.append(
        send(own_ref, all_ref.at[grp], send_sem.at[high_count - 1], recv_sem.at[grp], "grp",
             grp + 1 - 2 * low)
    )
    all_ref[grp] = own_ref[...]
    return copies


def gather_relay(n_grp, all_ref, send_sem, recv_sem):
    grp = lax.axis_index("grp")
    high_count = n_grp // LOW
    high, low = grp // LOW, lax.rem(grp, LOW)
    copies = []
    for i in range(1, high_count):
        block = lax.rem(high + high_count - i, high_count) * LOW + low
        arrived(all_ref.at[block], recv_sem.at[block])
        copies.append(
            send(all_ref.at[block], all_ref.at[block], send_sem.at[high_count - 1 + i],
                 recv_sem.at[block], "grp", grp + 1 - 2 * low)
        )
    return copies


def gather_finish(n_grp, all_ref, recv_sem):
    low = lax.rem(lax.axis_index("grp"), LOW)
    for h in range(n_grp // LOW):
        block = h * LOW + 1 - low
        arrived(all_ref.at[block], recv_sem.at[block])


def reduce_scatter(n_seq, rows_ref, w_ref, fetch, own_ref, y_send, y_recv, z_send, z_recv, sems,
                   finish):
    ys_sem, yr_sem, zs_sem, zr_sem = sems
    pieces, _, width = w_ref.shape
    seq = lax.axis_index("seq")
    high_count = n_seq // LOW
    high, low = seq // LOW, lax.rem(seq, LOW)
    half = rows_ref.shape[0] // LOW
    row_share = half // high_count
    wire = y_send.dtype

    def y_copy(p):
        return pltpu.make_async_remote_copy(
            src_ref=y_send.at[p], dst_ref=y_recv.at[p], send_sem=ys_sem.at[p],
            recv_sem=yr_sem.at[p], device_id={"seq": seq + 1 - 2 * low}, device_id_type=MESH)

    def z_copy(p, i):
        peer = lax.rem(high + i, high_count)
        return pltpu.make_async_remote_copy(
            src_ref=z_send.at[p, peer], dst_ref=z_recv.at[p, i - 1], send_sem=zs_sem.at[p, i - 1],
            recv_sem=zr_sem.at[p, i - 1], device_id={"seq": peer * LOW + low},
            device_id_type=MESH)

    def multiply(p, carry):
        fetch(p).wait()
        theirs = rows_ref[pl.ds(pl.multiple_of((1 - low) * half, half), half), :]
        y_send[p] = jnp.dot(theirs, w_ref[p], preferred_element_type=jnp.float32).astype(wire)
        y_copy(p).start()
        mine = rows_ref[pl.ds(pl.multiple_of(low * half, half), half), :]
        own_ref[p] = jnp.dot(mine, w_ref[p], preferred_element_type=jnp.float32).reshape(
            high_count, row_share, width
        )
        return carry

    def spread(p):
        y_copy(p).wait_recv()
        summed = own_ref[p] + y_recv[p].astype(jnp.float32).reshape(high_count, row_share, width)
        own_ref[p] = summed
        z_send[p] = summed.astype(wire)
        for i in range(1, high_count):
            z_copy(p, i).start()

    def collect(p):
        total = own_ref[p, high]
        for i in range(1, high_count):
            z_copy(p, i).wait_recv()
            total = total + z_recv[p, i - 1].astype(jnp.float32)
        finish(p, total)

    def step(p, carry):
        spread(p)
        collect(p - 1)
        return carry

    def drain(p, carry):
        y_copy(p).wait_send()
        for i in range(1, high_count):
            z_copy(p, i).wait_send()
        return carry

    lax.fori_loop(0, pieces, multiply, 0)
    spread(0)
    lax.fori_loop(1, pieces, step, 0)
    collect(pieces - 1)
    return lambda: lax.fori_loop(0, pieces, drain, 0)


def step_kernel(n_seq, n_grp, owner_ref, live_ref, hidden_ref, perm_ref, back_ref, bias_ref,
                cos_ref, sin_ref, w_in_hbm, w_out_hbm, k_hbm, v_hbm, mixed_ref,
                key_ref, value_ref, w_in_ref, w_out_ref, hid_all, rows_ref, p_own, p_ys, p_yr,
                p_zs, p_zr, turned_ref, d_send, d_recv, x_ref, wide_ref, block_ref, q_ref, nv_send,
                nv_ref, page_ref, stat_ref, o_send, o_all, s_all, att_ref, att_all, m_own, m_ys,
                m_yr, m_zs, m_zr, w_in_sem, w_out_sem, kv_sem, hs_sem, hr_sem, p_ys_sem, p_yr_sem,
                p_zs_sem, p_zr_sem, ds_sem, dr_sem, qs_sem, qf_sem, qr_sem, ns_sem, nr_sem, os_sem,
                or_sem, ss_sem, sr_sem, as_sem, ar_sem, m_ys_sem, m_yr_sem, m_zs_sem, m_zr_sem):
    seq, grp = lax.axis_index("seq"), lax.axis_index("grp")
    high_count = n_seq // LOW
    high, low = seq // LOW, lax.rem(seq, LOW)
    pair = seq + 1 - 2 * low
    in_pieces, depth, in_width = w_in_ref.shape
    out_pieces, out_depth, out_width = w_out_ref.shape
    parts = hid_all.shape[0]
    share = block_ref.shape[0]
    piece_heads = in_width // HD
    block_heads = in_pieces * piece_heads
    head_share = HQ // n_seq
    group_q = HQ // KVH
    group_size = share * n_seq

    def in_fetch(p):
        return pltpu.make_async_copy(
            w_in_hbm.at[:, pl.ds(pl.multiple_of(p * in_width, in_width), in_width)],
            w_in_ref.at[p], w_in_sem.at[p])

    def out_fetch(p):
        return pltpu.make_async_copy(
            w_out_hbm.at[:, pl.ds(pl.multiple_of(p * out_width, out_width), out_width)],
            w_out_ref.at[p], w_out_sem.at[p])

    key_copy = pltpu.make_async_copy(k_hbm.at[0], key_ref, kv_sem.at[0])
    value_copy = pltpu.make_async_copy(v_hbm.at[0], value_ref, kv_sem.at[1])
    for p in range(in_pieces):
        in_fetch(p).start()
    greet(n_seq, n_grp)

    sends = []
    part = depth // parts
    for a in range(parts):
        sends += gather_start(n_grp, hidden_ref.at[:, a * part : (a + 1) * part], hid_all.at[a],
                              hs_sem.at[a], hr_sem.at[a])
    key_copy.start()
    value_copy.start()
    for p in range(out_pieces):
        out_fetch(p).start()
    for a in range(parts):
        sends += gather_relay(n_grp, hid_all.at[a], hs_sem.at[a], hr_sem.at[a])
    for a in range(parts):
        gather_finish(n_grp, hid_all.at[a], hr_sem.at[a])
        rows_ref[:, a * part : (a + 1) * part] = jnp.dot(
            perm_ref[...], hid_all[a].reshape(-1, part), preferred_element_type=jnp.float32
        ).astype(jnp.bfloat16)

    def turn(p, total):
        for k in range(piece_heads):
            head = p * piece_heads + k
            values = total[:, k * HD : (k + 1) * HD] + bias_ref[pl.ds(head, 1), :]
            rotated = values * cos_ref[...] + pltpu.roll(values, HD // 2, 1) * sin_ref[...]
            values = jnp.where(grp * block_heads + head < HQ + KVH, rotated, values)
            for g in range(n_grp):
                turned_ref[g, pl.ds(head, share, stride=block_heads), :] = values[
                    g * share : (g + 1) * share
                ]

    drain_in = reduce_scatter(n_seq, rows_ref, w_in_ref, in_fetch, p_own, p_ys, p_yr, p_zs, p_zr,
                              (p_ys_sem, p_yr_sem, p_zs_sem, p_zr_sem), turn)

    d_send[...] = turned_ref[...].astype(jnp.bfloat16)
    head_sends = []
    for i in range(1, n_grp):
        peer = lax.rem(grp + i, n_grp)
        head_sends.append(
            send(d_send.at[peer], d_recv.at[i - 1], ds_sem.at[i - 1], dr_sem.at[i - 1], "grp", peer)
        )
    x_ref[grp] = d_send[grp].astype(jnp.float32)
    for i in range(1, n_grp):
        head_sends[i - 1].wait_recv()
        x_ref[lax.rem(grp + n_grp - i, n_grp)] = d_recv[i - 1].astype(jnp.float32)
    sends += head_sends

    def head_rows(head):
        return x_ref[head // block_heads, pl.ds(head % block_heads, share, stride=block_heads), :]

    for head in range(HQ):
        wide_ref[pl.ds(head, share, stride=HQ), :] = head_rows(head)
    block_ref[...] = wide_ref[...].reshape(share, HQ, HD).astype(jnp.bfloat16)

    chunks = qr_sem.shape[1]
    chunk = share // chunks

    def rows_of(index, c):
        return q_ref.at[pl.ds(index * share + c * chunk, chunk)]

    for c in range(chunks):
        source = block_ref.at[pl.ds(c * chunk, chunk)]
        for i in range(1, high_count):
            peer = lax.rem(high + i, high_count) * LOW + low
            sends.append(send(source, rows_of(seq, c), qs_sem.at[i - 1, c], qr_sem.at[seq, c],
                              "seq", peer))
        sends.append(send(source, rows_of(seq, c), qs_sem.at[high_count - 1, c], qr_sem.at[seq, c],
                          "seq", pair))
    q_ref[pl.ds(seq * share, share)] = block_ref[...]
    for c in range(chunks):
        for i in range(1, high_count):
            block = lax.rem(high + high_count - i, high_count) * LOW + low
            arrived(rows_of(block, c), qr_sem.at[block, c])
            sends.append(send(rows_of(block, c), rows_of(block, c), qf_sem.at[i - 1, c],
                              qr_sem.at[block, c], "seq", pair))

    lane = lax.broadcasted_iota(jnp.int32, (share, HD), 1)
    for peer in range(n_seq):
        kv = peer * head_share // group_q
        scores = jnp.zeros((share, HD), jnp.float32)
        for k in range(head_share):
            head = peer * head_share + k
            key = head_rows(HQ + head // group_q)
            score = jnp.sum(head_rows(head) * key, axis=1, keepdims=True) * (HD**-0.5)
            scores = jnp.where(lane == k, score, scores)
        nv_send[peer, 0] = scores
        nv_send[peer, 1] = head_rows(HQ + KVH + kv)
    for i in range(1, n_seq):
        peer = lax.rem(seq + i, n_seq)
        sends.append(
            send(nv_send.at[peer], nv_ref.at[seq], ns_sem.at[i - 1], nr_sem.at[seq], "seq", peer)
        )
    nv_ref[seq] = nv_send[seq]
    stat_ref[...] = jnp.zeros_like(stat_ref)
    key_copy.wait()
    value_copy.wait()
    for h in range(high_count):
        for c in range(chunks):
            block = h * LOW + 1 - low
            arrived(rows_of(block, c), qr_sem.at[block, c])

    blocks, block_rows, _ = o_send.shape
    block_pages = block_rows // HQ
    pool_pages = blocks * block_pages
    unroll = math.gcd(block_pages, 8)
    place = lax.broadcasted_iota(jnp.int32, (HQ, PAGE), 1)
    spot = lax.broadcasted_iota(jnp.int32, (HQ, HD), 1)
    own_rows = head_share * block_pages

    def attend(first, step, carry):
        stat = stat_ref[...].reshape(HQ, HD)
        for j in range(unroll):
            within = step * unroll + j
            page = first + within
            alive = place < live_ref[page]
            query = q_ref[owner_ref[page]]
            start = pl.multiple_of(page * PAGE, PAGE)
            keys = key_ref[pl.ds(start, PAGE), :]
            values = value_ref[pl.ds(start, PAGE), :]
            scores = jnp.concatenate(
                [
                    lax.dot_general(
                        query[h * group_q : (h + 1) * group_q],
                        keys[:, h * HD : (h + 1) * HD],
                        (((1,), (1,)), ((), ())),
                        preferred_element_type=jnp.float32,
                    )
                    for h in range(KVH)
                ],
                axis=0,
            ) * (HD**-0.5)
            scores = jnp.where(alive, scores, neg_fill)
            page_max = jnp.max(scores, axis=1, keepdims=True)
            weights = jnp.where(alive, jnp.exp(scores - page_max), 0.0)
            page_total = jnp.sum(weights, axis=1, keepdims=True)
            rounded = weights.astype(jnp.bfloat16)
            page_out = jnp.concatenate(
                [
                    jnp.dot(
                        rounded[h * group_q : (h + 1) * group_q],
                        values[:, h * HD : (h + 1) * HD],
                        preferred_element_type=jnp.float32,
                    )
                    for h in range(KVH)
                ],
                axis=0,
            )
            page_ref[pl.ds(within, HQ, stride=block_pages), :] = page_out
            holder = jnp.where(live_ref[page] > 0, owner_ref[page], -1).astype(jnp.float32)
            stat = jnp.where(spot == page, page_max, stat)
            stat = jnp.where(spot == pool_pages + page, page_total, stat)
            stat = jnp.where(spot == 2 * pool_pages + page, holder, stat)
        stat_ref[...] = stat.reshape(stat_ref.shape)
        return carry

    for b in range(blocks):
        lax.fori_loop(
            0, block_pages // unroll, functools.partial(attend, b * block_pages), 0
        )
        o_send[b] = page_ref[...].astype(jnp.bfloat16)
        for i in range(1, n_seq):
            peer = lax.rem(seq + i, n_seq)
            if b == blocks - 1:
                sends.append(send(stat_ref.at[peer], s_all.at[seq], ss_sem.at[i - 1],
                                  sr_sem.at[seq], "seq", peer))
            sends.append(send(o_send.at[b, pl.ds(peer * own_rows, own_rows)], o_all.at[seq, b],
                              os_sem.at[i - 1, b], or_sem.at[seq, b], "seq", peer))
        o_all[seq, b] = o_send[b, pl.ds(pl.multiple_of(seq * own_rows, own_rows), own_rows)]
    s_all[seq] = stat_ref[seq]

    for i in range(1, n_seq):
        block = lax.rem(seq + i, n_seq)
        arrived(nv_ref.at[block], nr_sem.at[block])
        arrived(s_all.at[block], sr_sem.at[block])
    packed = HD // pool_pages
    slots = n_seq * pool_pages
    spot = lax.broadcasted_iota(jnp.int32, (head_share, HD), 1) // pool_pages

    def lined_up(field):
        tiles = []
        for first in range(0, n_seq, packed):
            tile = jnp.zeros((head_share, HD), jnp.float32)
            for k in range(packed):
                shift = (HD + (k - field) * pool_pages) % HD
                source = s_all[first + k]
                tile = jnp.where(spot == k, pltpu.roll(source, shift, 1) if shift else source, tile)
            tiles.append(tile)
        return jnp.concatenate(tiles, axis=1)

    tops, totals, holders = lined_up(0), lined_up(1), lined_up(2)
    request = lax.broadcasted_iota(jnp.int32, (group_size, slots), 0).astype(jnp.float32)
    held = request == holders[:1, :]
    fresh_scores = nv_ref[:, 0].reshape(group_size, HD)
    fresh_values = nv_ref[:, 1].reshape(group_size, HD)
    for b in range(blocks):
        for i in range(1, n_seq):
            block = lax.rem(seq + i, n_seq)
            arrived(o_all.at[block, b], or_sem.at[block, b])
    parts = att_all.shape[0]
    part_heads = head_share // parts
    part = part_heads * HD
    for a in range(parts):
        for m in range(part_heads):
            k = a * part_heads + m
            top = jnp.where(held, tops[k : k + 1, :], neg_fill)
            fresh = fresh_scores[:, k : k + 1]
            peak = jnp.maximum(jnp.max(top, axis=1, keepdims=True), fresh)
            factor = jnp.where(held, jnp.exp(top - peak), 0.0)
            fresh_weight = jnp.exp(fresh - peak)
            denominator = (
                jnp.sum(factor * totals[k : k + 1, :], axis=1, keepdims=True) + fresh_weight
            )
            coarse = factor.astype(jnp.bfloat16)
            fine = (factor - coarse.astype(jnp.float32)).astype(jnp.bfloat16)
            outs = o_all[:, :, k * block_pages : (k + 1) * block_pages, :].reshape(slots, HD)
            numerator = (
                jnp.dot(coarse, outs, preferred_element_type=jnp.float32)
                + jnp.dot(fine, outs, preferred_element_type=jnp.float32)
                + fresh_weight * fresh_values
            )
            att_ref[a, :, m * HD : (m + 1) * HD] = (numerator / denominator).astype(jnp.bfloat16)
        sends += gather_start(n_grp, att_ref.at[a], att_all.at[a], as_sem.at[a], ar_sem.at[a])
    for a in range(parts):
        sends += gather_relay(n_grp, att_all.at[a], as_sem.at[a], ar_sem.at[a])
    for a in range(parts):
        gather_finish(n_grp, att_all.at[a], ar_sem.at[a])
        rows_ref[:, a * part : (a + 1) * part] = jnp.dot(
            back_ref[...], att_all[a].reshape(-1, part), preferred_element_type=jnp.float32
        ).astype(jnp.bfloat16)

    def keep(p, total):
        mixed_ref[:, pl.ds(pl.multiple_of(p * out_width, out_width), out_width)] = total.astype(
            jnp.bfloat16
        )

    drain_out = reduce_scatter(n_seq, rows_ref.at[:, :out_depth], w_out_ref, out_fetch, m_own,
                               m_ys, m_yr, m_zs, m_zr, (m_ys_sem, m_yr_sem, m_zs_sem, m_zr_sem),
                               keep)
    drain_in()
    drain_out()
    for copy in sends:
        copy.wait_send()


def run_step(n_seq, n_grp, owner, live, hidden, perm, back, bias, cosine, sine, w_qkv, w_out,
             k_cache, v_cache):
    group_size, depth = hidden.shape
    request_total = perm.shape[0]
    in_cols = w_qkv.shape[1]
    out_depth, out_cols = w_out.shape
    in_pieces, out_pieces = math.gcd(in_cols // HD, 10), math.gcd(out_cols // HD, 8)
    in_width, out_width = in_cols // in_pieces, out_cols // out_pieces
    half = request_total // LOW
    high_count = n_seq // LOW
    row_share = half // high_count
    share = row_share // n_grp
    head_share = HQ // n_seq
    block_rows = share * in_cols // HD
    positions = k_cache.shape[1]
    pool_pages = positions // PAGE
    block_pages = math.gcd(pool_pages, 16)
    blocks = pool_pages // block_pages
    chunks = math.gcd(share, 4)
    parts = 2
    bf16, f32 = jnp.bfloat16, jnp.float32
    dma = pltpu.SemaphoreType.DMA
    vmem = pl.BlockSpec(memory_space=pltpu.VMEM)
    smem = pl.BlockSpec(memory_space=pltpu.SMEM)
    hbm = pl.BlockSpec(memory_space=pl.ANY)
    scratch = [
        ((positions, KVH * HD), bf16),
        ((positions, KVH * HD), bf16),
        ((in_pieces, depth, in_width), bf16),
        ((out_pieces, out_depth, out_width), bf16),
        ((parts, n_grp, group_size, depth // parts), bf16),
        ((request_total, max(depth, out_depth)), bf16),
        ((in_pieces, high_count, row_share, in_width), f32),
        ((in_pieces, half, in_width), f32),
        ((in_pieces, half, in_width), f32),
        ((in_pieces, high_count, row_share, in_width), f32),
        ((in_pieces, high_count - 1, row_share, in_width), f32),
        ((n_grp, block_rows, HD), f32),
        ((n_grp, block_rows, HD), bf16),
        ((n_grp - 1, block_rows, HD), bf16),
        ((n_grp, block_rows, HD), f32),
        ((share * HQ, HD), f32),
        ((share, HQ, HD), bf16),
        ((group_size, HQ, HD), bf16),
        ((n_seq, 2, share, HD), f32),
        ((n_seq, 2, share, HD), f32),
        ((HQ * block_pages, HD), f32),
        ((n_seq, head_share, HD), f32),
        ((blocks, HQ * block_pages, HD), bf16),
        ((n_seq, blocks, head_share * block_pages, HD), bf16),
        ((n_seq, head_share, HD), f32),
        ((parts, group_size, out_depth // parts), bf16),
        ((parts, n_grp, group_size, out_depth // parts), bf16),
        ((out_pieces, high_count, row_share, out_width), f32),
        ((out_pieces, half, out_width), bf16),
        ((out_pieces, half, out_width), bf16),
        ((out_pieces, high_count, row_share, out_width), bf16),
        ((out_pieces, high_count - 1, row_share, out_width), bf16),
    ]
    sems = [
        (in_pieces,), (out_pieces,), (2,), (parts, 2 * n_grp), (parts, n_grp),
        (in_pieces,), (in_pieces,), (in_pieces, high_count - 1), (in_pieces, high_count - 1),
        (n_grp - 1,), (n_grp - 1,), (high_count, chunks), (high_count - 1, chunks),
        (n_seq, chunks), (n_seq - 1,), (n_seq,), (n_seq - 1, blocks), (n_seq, blocks),
        (n_seq - 1,), (n_seq,), (parts, 2 * n_grp), (parts, n_grp),
        (out_pieces,), (out_pieces,), (out_pieces, high_count - 1), (out_pieces, high_count - 1),
    ]
    return pl.pallas_call(
        functools.partial(step_kernel, n_seq, n_grp),
        out_shape=jax.ShapeDtypeStruct((row_share, out_cols), bf16),
        in_specs=[smem, smem] + [vmem] * 6 + [hbm] * 4,
        out_specs=vmem,
        scratch_shapes=[pltpu.VMEM(s, t) for s, t in scratch] + [dma(s) for s in sems],
        compiler_params=pltpu.CompilerParams(
            collective_id=0, has_side_effects=True, vmem_limit_bytes=60 * 1024 * 1024
        ),
        cost_estimate=pl.CostEstimate(
            flops=2 * request_total * depth * in_cols,
            bytes_accessed=2 * depth * in_cols,
            transcendentals=0,
        ),
    )(owner, live, hidden, perm, back, bias, cosine, sine, w_qkv, w_out, k_cache, v_cache)


def rope_tables(places):
    freq_index = jnp.arange(HD // 2, dtype=jnp.int32)
    inverse_freq = jnp.exp(freq_index.astype(jnp.float32) * (-2.0 * math.log(rope_base) / HD))
    section = jnp.where(
        freq_index < HD // 8, 0, jnp.where(freq_index < HD // 8 + 3 * HD // 16, 1, 2)
    )
    place_float = places.astype(jnp.float32)
    chosen = jnp.where(
        section[None, :] == 0,
        place_float[0][:, None],
        jnp.where(section[None, :] == 1, place_float[1][:, None], place_float[2][:, None]),
    )
    angles = chosen * inverse_freq[None, :]
    cosine, sine = jnp.cos(angles), jnp.sin(angles)
    return jnp.concatenate([cosine, cosine], 1), jnp.concatenate([-sine, sine], 1)


def shards(hidden, w_qkv, b_qkv, w_out, k_cache, v_cache, lengths, page_table, positions, group_of):
    n_seq = lax.axis_size("seq")
    n_grp = lax.axis_size("grp")
    seq_index = lax.axis_index("seq")
    grp_index = lax.axis_index("grp")
    request_total = group_of.shape[0]
    group_size = request_total // n_grp
    share = group_size // n_seq
    high_count = n_seq // LOW
    row_share = request_total // n_seq
    request_ids = jnp.arange(request_total, dtype=jnp.int32)
    before = (group_of[None, :] < group_of[:, None]) | (group_of[None, :] == group_of[:, None]) & (
        request_ids[None, :] < request_ids[:, None]
    )
    served_at = jnp.sum(before.astype(jnp.int32), axis=1)
    rank = served_at % group_size
    holder = rank // share
    sent_at = (
        ((holder % LOW) * high_count + holder // LOW) * n_grp + served_at // group_size
    ) * share + rank % share
    in_perm = sent_at[None, :] == request_ids[:, None]
    my_start = ((seq_index % LOW) * high_count + seq_index // LOW) * row_share
    my_rows = (
        my_start + jnp.arange(row_share, dtype=jnp.int32)[:, None] == sent_at[None, :]
    )
    places = jnp.sum(jnp.where(my_rows[None], positions[:, None, :], 0), axis=2)
    cosine, sine = rope_tables(places)
    placed_at = served_at[None, :] == request_ids[:, None]
    served_order = jnp.sum(jnp.where(placed_at, request_ids[None, :], 0), axis=1)
    served_ids = lax.dynamic_slice_in_dim(served_order, grp_index * group_size, group_size, 0)
    served_len = lengths[served_ids]
    served_table = page_table[served_ids]
    most_pages = page_table.shape[1]
    page_counts = (served_len + PAGE - 1) // PAGE
    logical = jnp.arange(most_pages, dtype=jnp.int32)
    pool_pages = k_cache.shape[1] // PAGE
    local_page = served_table - seq_index * pool_pages
    usable = (
        (logical[None, :] < page_counts[:, None]) & (local_page >= 0) & (local_page < pool_pages)
    )
    pool_ids = jnp.arange(pool_pages, dtype=jnp.int32)
    matched = usable[:, :, None] & (local_page[:, :, None] == pool_ids[None, None, :])
    owner_ids = jnp.arange(group_size, dtype=jnp.int32)
    left = served_len[:, None] - logical[None, :] * PAGE
    live = jnp.max(jnp.where(matched, left[:, :, None], 0), axis=(0, 1))
    owner = jnp.max(jnp.where(matched, owner_ids[:, None, None], 0), axis=(0, 1))
    back_at = served_at.reshape(high_count, LOW, row_share).transpose(1, 0, 2).reshape(-1)
    out_perm = back_at[:, None] == request_ids[None, :]
    return run_step(
        n_seq, n_grp, owner, live, hidden, in_perm.astype(jnp.bfloat16),
        out_perm.astype(jnp.bfloat16), b_qkv.reshape(-1, HD), cosine, sine, w_qkv, w_out, k_cache,
        v_cache
    )


def solution(mesh):
    placed = (
        P("grp", "seq"),
        P("seq", "grp"),
        P("grp"),
        P("seq", "grp"),
        P("grp", "seq", None),
        P("grp", "seq", None),
        P(),
        P(),
        P(),
        P(),
    )
    return jax.shard_map(
        shards, mesh=mesh, in_specs=placed, out_specs=P("seq", "grp"), check_vma=False
    )
```

time: 242 us -> 129 us (0.53)
  waiting for transfers between devices: 107 us -> 0 us
  Pallas kernels: 20.5 us -> 119 us
  blocking collectives: 52.5 us -> 0 us
  local copies, waits for them, and re-layouts: 23.8 us -> 3.82 us
  starting transfers between devices: 17 us -> 0 us
  matrix products: 8.95 us -> 0 us
  other arithmetic: 11.7 us -> 5.07 us
    all_to_all x4 -> x0, waiting for transfers between devices: 107 us -> none  [the longest x1 58.5 us: shards(): lax.all_to_all(partial_sum.reshape(seq_count, row_share, col_count), 'seq...]
    pallas_call x1, Pallas kernels: 20.5 us -> 119 us  [run_step(): pl.pallas_call(functools.partial(step_kernel, n_seq, n_grp), out_shape=ja...]
    all_to_all x2 -> x0, blocking collectives: 37.2 us -> none  [the longest x1 29.9 us: shards(): lax.all_to_all(mixed.reshape(seq_count, row_share, mixed.shape[1]), 'seq'...]
    all_to_all x4 -> x0, starting transfers between devices: 17 us -> none  [the longest x1 5.97 us: shards(): lax.all_to_all(partial_sum.reshape(seq_count, row_share, col_count), 'seq...]
    all_gather x2 -> x0, blocking collectives: 15.4 us -> none  [the longest x1 8.86 us: shards(): hidden_all = lax.all_gather(hidden, 'grp', axis=0, tiled=True)[send_order]]
    dot_general x2 -> x0, matrix products: 8.95 us -> none  [the longest x1 5.51 us: shards(): partial_sum = jnp.dot(hidden_all, w_qkv, preferred_element_type=jnp.float32)]
    slice x4 -> x0, local copies, waits for them, and re-layouts: 8.35 us -> none  [the longest x3 8.18 us: shards(): stats = jnp.stack([local_stat[:, :, 0], local_stat[:, :, HD // 2]], axis=0)]
    convert_element_type x5 -> x2, other arithmetic: 5.09 us -> 0.75 us  [the longest x1 0.74 us: shards(): in_perm.astype(jnp.bfloat16)]
  transfers between devices with their start and end apart: 4 -> 0, of which waited for: 4 -> 0; matrix products, arithmetic and copies ran while one was open for 7% -> 0% of each run, Pallas kernels for 0% -> 0%
where the time goes in v2:
time: 129 us; the launch traced here: 128 us
  Pallas kernels  119 us (92%)
  other arithmetic  5.07 us (4%)
  local copies, waits for them, and re-layouts  3.82 us (3%)
    pallas_call x1, Pallas kernels, run_step(): pl.pallas_call(functools.partial(step_kernel, n_seq, n_grp), out_shape=ja...  119 us

profile of v2, /device:TPU:0, one launch (start us, length us, event | category | flops | bytes accessed | tf_op | source)
XLA Modules:
  0.0 128.3 jit_solution(559600394944312916)
XLA Ops:
  0.0 0.0 copy-start
  0.1 0.9 convert_reduce_fusion
  1.0 0.1 select_reduce_fusion.2
  1.2 0.1 compare_select_fusion
  1.2 0.1 reshape.232
  1.3 0.1 eq.106
  1.4 1.5 %gather_fusion = s32[64]{0:T(128)S(1)} fusion(s32[256]{0:T(256)} %param.16, s32[1024]{0:T(1024)S(1)} %pad_clamp_fusion), kind=kCustom, calls=%fused_computation | custom fusion | bytes 768 | tf_op jit(solution)/shard_map/gather | solution.py:569
  2.9 0.1 broadcast_compare_fusion
  3.0 0.8 select_reduce_fusion.3
  3.8 0.0 copy-done
  3.8 0.6 gather_fusion.1
  4.4 0.1 fusion.6
  4.5 0.1 broadcast_subtract_fusion
  4.6 1.2 select_reduce_fusion
  5.8 0.1 fusion.13
  6.0 0.7 pad_maximum_fusion
  6.6 0.7 fusion.3
  7.4 119.3 %shard_map.100 = bf16[32,2048]{1,0:T(8,128)(2,1)} custom-call(s32[32]{0:T(128)} %get-tuple-element.6.owner_ref, s32[32]{0:T(128)} %get-tuple-element.5.live_ref, bf16[64,1024]{1,0:T(8,128)(2,1)} %hidden_ref.1, bf16[256,256]{1,0:T(8,128)(2,1)} %get-tuple-element.17.perm_ref, bf16[256,256]{1,0:T(8,128)(2,1)} %get-tuple-element.18.back_ref, f32[20,128]{1,0:T(8,128)} %bitcast.9, ...), custom_call_target="tpu_custom_call" | custom-call | flops 1342177280 | bytes 5242880 | tf_op jit(solution)/shard_map/pallas_call | solution.py:505
  126.7 1.6 %copy.14 = bf16[32,2048]{1,0:T(8,128)(2,1)} copy(bf16[32,2048]{1,0:T(8,128)(2,1)} %shard_map.100) | data formatting | bytes 262144
  (11 shorter events, 0.1 us)
Async XLA Ops:
  0.0 3.8 %copy-start = (s32[256,128]{1,0:T(8,128)S(1)}, s32[256,128]{1,0:T(8,128)}, u32[]{:S(2)}) copy-start(s32[256,128]{1,0:T(8,128)} %param.17) | copy-start | bytes 393220

commit v3 on v2

--- a/solution.py
+++ b/solution.py
@@ -30,7 +30,94 @@
         pl.semaphore_signal(
             barrier, inc=1, device_id={"grp": lax.rem(grp + i, n_grp)}, device_id_type=MESH
         )
-    pl.semaphore_wait(barrier, n_seq + n_grp - 2)
+
+
+def greeted(n_seq, n_grp):
+    pl.semaphore_wait(pltpu.get_barrier_semaphore(), n_seq + n_grp - 2)
+
+
+def split_exact(values):
+    terms = []
+    for _ in range(3):
+        terms.append(values.astype(jnp.bfloat16))
+        values = values - terms[-1].astype(jnp.float32)
+    return terms
+
+
+def row_col(shape):
+    return tuple(lax.broadcasted_iota(jnp.int32, shape, d).astype(jnp.float32) for d in (0, 1))
+
+
+def one_hot(mask):
+    return mask.astype(jnp.float32).astype(jnp.bfloat16)
+
+
+def whole_part(values, divisor):
+    return jnp.floor((values + 0.5) * (1.0 / divisor))
+
+
+def serve_order(n_seq, n_grp, group_of_ref, perm_ref):
+    total = group_of_ref.shape[1]
+    group_size = total // n_grp
+    share = group_size // n_seq
+    row, col = row_col((total, total))
+    member = group_of_ref[...].astype(jnp.float32)
+    member_down = jnp.sum(jnp.where(row == col, member, 0.0), axis=1, keepdims=True)
+    earlier = (member_down < member) | ((member_down == member) & (row < col))
+    served = jnp.sum(jnp.where(earlier, 1.0, 0.0), axis=0, keepdims=True)
+    rank = served - member * group_size
+    holder = whole_part(rank, share)
+    high = whole_part(holder, LOW)
+    low = holder - high * LOW
+    sent = ((low * (n_seq // LOW) + high) * n_grp + member) * share + rank - holder * share
+    perm_ref[...] = one_hot(row == sent)
+    return served, sent
+
+
+def serve_tables(n_seq, n_grp, order, group_of_ref, len_ref, table_ref, cos_all_ref, sin_all_ref, back_ref,
+                 cos_ref, sin_ref, slot_ref):
+    served, sent = order
+    seq, grp = lax.axis_index("seq"), lax.axis_index("grp")
+    total = served.shape[1]
+    group_size = total // n_grp
+    row_share = total // n_seq
+    high_count = n_seq // LOW
+    pool_pages = slot_ref.shape[0]
+    row, col = row_col((total, total))
+    low_part = whole_part(row, total // LOW)
+    rest = row - low_part * (total // LOW)
+    high_part = whole_part(rest, row_share)
+    wanted = (high_part * LOW + low_part) * row_share + rest - high_part * row_share
+    served_down = jnp.sum(jnp.where(col == wanted, served, 0.0), axis=1, keepdims=True)
+    back_ref[...] = one_hot(col == served_down)
+
+    start = (lax.rem(seq, LOW) * high_count + seq // LOW) * row_share
+    row, _ = row_col((row_share, total))
+    mine = one_hot(row + start.astype(jnp.float32) == sent)
+    for source, target in ((cos_all_ref, cos_ref), (sin_all_ref, sin_ref)):
+        target[...] = sum(
+            jnp.dot(mine, term, preferred_element_type=jnp.float32)
+            for term in split_exact(source[...])
+        )
+
+    row = lax.broadcasted_iota(jnp.int32, (total, total), 0)
+    col = lax.broadcasted_iota(jnp.int32, (total, total), 1)
+    member = group_of_ref[...]
+    member_down = jnp.sum(jnp.where(row == col, member, 0), axis=1, keepdims=True)
+    lengths = jnp.sum(jnp.where(row == col, len_ref[...], 0), axis=1, keepdims=True)
+    earlier = (member < member_down) | ((member == member_down) & (col < row))
+    rank_down = jnp.sum(jnp.where(earlier, 1, 0), axis=1, keepdims=True) - member_down * group_size
+    place = table_ref[...] - seq * pool_pages
+    left = lengths - lax.broadcasted_iota(jnp.int32, place.shape, 1) * PAGE
+    code = jnp.where((member_down == grp) & (left > 0), left * group_size + rank_down, 0)
+    codes = jnp.concatenate(
+        [
+            jnp.sum(jnp.where(place == p, code, 0), axis=0, keepdims=True)
+            for p in range(pool_pages)
+        ],
+        axis=0,
+    )
+    slot_ref[...] = jnp.broadcast_to(jnp.sum(codes, axis=1, keepdims=True), slot_ref.shape)
 
 
 def send(src, dst, send_sem, recv_sem, axis, index):
@@ -90,7 +177,7 @@
 
 
 def reduce_scatter(n_seq, rows_ref, w_ref, fetch, own_ref, y_send, y_recv, z_send, z_recv, sems,
-                   finish):
+                   finish, lag):
     ys_sem, yr_sem, zs_sem, zr_sem = sems
     pieces, _, width = w_ref.shape
     seq = lax.axis_index("seq")
@@ -138,9 +225,17 @@
             total = total + z_recv[p, i - 1].astype(jnp.float32)
         finish(p, total)
 
+    def first(p, carry):
+        spread(p)
+        return carry
+
     def step(p, carry):
         spread(p)
-        collect(p - 1)
+        collect(p - lag)
+        return carry
+
+    def last(p, carry):
+        collect(p)
         return carry
 
     def drain(p, carry):
@@ -150,18 +245,20 @@
         return carry
 
     lax.fori_loop(0, pieces, multiply, 0)
-    spread(0)
-    lax.fori_loop(1, pieces, step, 0)
-    collect(pieces - 1)
+    lag = min(lag, pieces)
+    lax.fori_loop(0, lag, first, 0)
+    lax.fori_loop(lag, pieces, step, 0)
+    lax.fori_loop(pieces - lag, pieces, last, 0)
     return lambda: lax.fori_loop(0, pieces, drain, 0)
 
 
-def step_kernel(n_seq, n_grp, owner_ref, live_ref, hidden_ref, perm_ref, back_ref, bias_ref,
-                cos_ref, sin_ref, w_in_hbm, w_out_hbm, k_hbm, v_hbm, mixed_ref,
+def step_kernel(n_seq, n_grp, hidden_ref, group_of_ref, len_ref, table_ref, bias_ref,
+                cos_all_ref, sin_all_ref, w_in_hbm, w_out_hbm, k_hbm, v_hbm, mixed_ref,
+                perm_ref, back_ref, cos_ref, sin_ref, slot_ref, slots_ref,
                 key_ref, value_ref, w_in_ref, w_out_ref, hid_all, rows_ref, p_own, p_ys, p_yr,
                 p_zs, p_zr, turned_ref, d_send, d_recv, x_ref, wide_ref, block_ref, q_ref, nv_send,
                 nv_ref, page_ref, stat_ref, o_send, o_all, s_all, att_ref, att_all, m_own, m_ys,
-                m_yr, m_zs, m_zr, w_in_sem, w_out_sem, kv_sem, hs_sem, hr_sem, p_ys_sem, p_yr_sem,
+                m_yr, m_zs, m_zr, slot_sem, w_in_sem, w_out_sem, kv_sem, hs_sem, hr_sem, p_ys_sem, p_yr_sem,
                 p_zs_sem, p_zr_sem, ds_sem, dr_sem, qs_sem, qf_sem, qr_sem, ns_sem, nr_sem, os_sem,
                 or_sem, ss_sem, sr_sem, as_sem, ar_sem, m_ys_sem, m_yr_sem, m_zs_sem, m_zr_sem):
     seq, grp = lax.axis_index("seq"), lax.axis_index("grp")
@@ -193,6 +290,8 @@
     for p in range(in_pieces):
         in_fetch(p).start()
     greet(n_seq, n_grp)
+    order = serve_order(n_seq, n_grp, group_of_ref, perm_ref)
+    greeted(n_seq, n_grp)
 
     sends = []
     part = depth // parts
@@ -203,6 +302,10 @@
     value_copy.start()
     for p in range(out_pieces):
         out_fetch(p).start()
+    serve_tables(n_seq, n_grp, order, group_of_ref, len_ref, table_ref, cos_all_ref, sin_all_ref, back_ref,
+                 cos_ref, sin_ref, slot_ref)
+    slot_copy = pltpu.make_async_copy(slot_ref, slots_ref, slot_sem)
+    slot_copy.start()
     for a in range(parts):
         sends += gather_relay(n_grp, hid_all.at[a], hs_sem.at[a], hr_sem.at[a])
     for a in range(parts):
@@ -223,7 +326,7 @@
                 ]
 
     drain_in = reduce_scatter(n_seq, rows_ref, w_in_ref, in_fetch, p_own, p_ys, p_yr, p_zs, p_zr,
-                              (p_ys_sem, p_yr_sem, p_zs_sem, p_zr_sem), turn)
+                              (p_ys_sem, p_yr_sem, p_zs_sem, p_zr_sem), turn, 2)
 
     d_send[...] = turned_ref[...].astype(jnp.bfloat16)
     head_sends = []
@@ -285,6 +388,7 @@
         )
     nv_ref[seq] = nv_send[seq]
     stat_ref[...] = jnp.zeros_like(stat_ref)
+    slot_copy.wait()
     key_copy.wait()
     value_copy.wait()
     for h in range(high_count):
@@ -305,8 +409,9 @@
         for j in range(unroll):
             within = step * unroll + j
             page = first + within
-            alive = place < live_ref[page]
-            query = q_ref[owner_ref[page]]
+            page_live, owner = slots_ref[page, 0] // group_size, slots_ref[page, 0] % group_size
+            alive = place < page_live
+            query = q_ref[owner]
             start = pl.multiple_of(page * PAGE, PAGE)
             keys = key_ref[pl.ds(start, PAGE), :]
             values = value_ref[pl.ds(start, PAGE), :]
@@ -339,7 +444,7 @@
                 axis=0,
             )
             page_ref[pl.ds(within, HQ, stride=block_pages), :] = page_out
-            holder = jnp.where(live_ref[page] > 0, owner_ref[page], -1).astype(jnp.float32)
+            holder = jnp.where(page_live > 0, owner, -1).astype(jnp.float32)
             stat = jnp.where(spot == page, page_max, stat)
             stat = jnp.where(spot == pool_pages + page, page_total, stat)
             stat = jnp.where(spot == 2 * pool_pages + page, holder, stat)
@@ -428,17 +533,17 @@
 
     drain_out = reduce_scatter(n_seq, rows_ref.at[:, :out_depth], w_out_ref, out_fetch, m_own,
                                m_ys, m_yr, m_zs, m_zr, (m_ys_sem, m_yr_sem, m_zs_sem, m_zr_sem),
-                               keep)
+                               keep, 8)
     drain_in()
     drain_out()
     for copy in sends:
         copy.wait_send()
 
 
-def run_step(n_seq, n_grp, owner, live, hidden, perm, back, bias, cosine, sine, w_qkv, w_out,
+def run_step(n_seq, n_grp, hidden, group_of, lengths, table, bias, cosine, sine, w_qkv, w_out,
              k_cache, v_cache):
     group_size, depth = hidden.shape
-    request_total = perm.shape[0]
+    request_total = table.shape[0]
     in_cols = w_qkv.shape[1]
     out_depth, out_cols = w_out.shape
     in_pieces, out_pieces = math.gcd(in_cols // HD, 10), math.gcd(out_cols // HD, 8)
@@ -451,16 +556,23 @@
     block_rows = share * in_cols // HD
     positions = k_cache.shape[1]
     pool_pages = positions // PAGE
-    block_pages = math.gcd(pool_pages, 16)
+    block_pages = math.gcd(pool_pages, 8)
     blocks = pool_pages // block_pages
     chunks = math.gcd(share, 4)
     parts = 2
     bf16, f32 = jnp.bfloat16, jnp.float32
     dma = pltpu.SemaphoreType.DMA
     vmem = pl.BlockSpec(memory_space=pltpu.VMEM)
-    smem = pl.BlockSpec(memory_space=pltpu.SMEM)
     hbm = pl.BlockSpec(memory_space=pl.ANY)
     scratch = [
+        ((request_total, request_total), bf16),
+        ((request_total, request_total), bf16),
+        ((row_share, HD), f32),
+        ((row_share, HD), f32),
+        ((pool_pages, HD), jnp.int32),
+    ]
+    smem_scratch = [pltpu.SMEM((pool_pages, HD), jnp.int32)]
+    more_scratch = [
         ((positions, KVH * HD), bf16),
         ((positions, KVH * HD), bf16),
         ((in_pieces, depth, in_width), bf16),
@@ -505,9 +617,13 @@
     return pl.pallas_call(
         functools.partial(step_kernel, n_seq, n_grp),
         out_shape=jax.ShapeDtypeStruct((row_share, out_cols), bf16),
-        in_specs=[smem, smem] + [vmem] * 6 + [hbm] * 4,
+        in_specs=[vmem] * 7 + [hbm] * 4,
         out_specs=vmem,
-        scratch_shapes=[pltpu.VMEM(s, t) for s, t in scratch] + [dma(s) for s in sems],
+        scratch_shapes=[pltpu.VMEM(s, t) for s, t in scratch]
+        + smem_scratch
+        + [pltpu.VMEM(s, t) for s, t in more_scratch]
+        + [dma(())]
+        + [dma(s) for s in sems],
         compiler_params=pltpu.CompilerParams(
             collective_id=0, has_side_effects=True, vmem_limit_bytes=60 * 1024 * 1024
         ),
@@ -516,78 +632,33 @@
             bytes_accessed=2 * depth * in_cols,
             transcendentals=0,
         ),
-    )(owner, live, hidden, perm, back, bias, cosine, sine, w_qkv, w_out, k_cache, v_cache)
-
-
-def rope_tables(places):
-    freq_index = jnp.arange(HD // 2, dtype=jnp.int32)
+    )(hidden, group_of, lengths, table, bias, cosine, sine, w_qkv, w_out, k_cache, v_cache)
+
+
+def rope_tables(positions):
+    column = jnp.arange(HD, dtype=jnp.int32)
+    freq_index = column % (HD // 2)
     inverse_freq = jnp.exp(freq_index.astype(jnp.float32) * (-2.0 * math.log(rope_base) / HD))
     section = jnp.where(
         freq_index < HD // 8, 0, jnp.where(freq_index < HD // 8 + 3 * HD // 16, 1, 2)
     )
-    place_float = places.astype(jnp.float32)
+    place_float = positions.astype(jnp.float32)
     chosen = jnp.where(
         section[None, :] == 0,
         place_float[0][:, None],
         jnp.where(section[None, :] == 1, place_float[1][:, None], place_float[2][:, None]),
     )
     angles = chosen * inverse_freq[None, :]
-    cosine, sine = jnp.cos(angles), jnp.sin(angles)
-    return jnp.concatenate([cosine, cosine], 1), jnp.concatenate([-sine, sine], 1)
+    sine = jnp.sin(angles)
+    return jnp.cos(angles), jnp.where((column < HD // 2)[None, :], -sine, sine)
 
 
 def shards(hidden, w_qkv, b_qkv, w_out, k_cache, v_cache, lengths, page_table, positions, group_of):
-    n_seq = lax.axis_size("seq")
-    n_grp = lax.axis_size("grp")
-    seq_index = lax.axis_index("seq")
-    grp_index = lax.axis_index("grp")
-    request_total = group_of.shape[0]
-    group_size = request_total // n_grp
-    share = group_size // n_seq
-    high_count = n_seq // LOW
-    row_share = request_total // n_seq
-    request_ids = jnp.arange(request_total, dtype=jnp.int32)
-    before = (group_of[None, :] < group_of[:, None]) | (group_of[None, :] == group_of[:, None]) & (
-        request_ids[None, :] < request_ids[:, None]
-    )
-    served_at = jnp.sum(before.astype(jnp.int32), axis=1)
-    rank = served_at % group_size
-    holder = rank // share
-    sent_at = (
-        ((holder % LOW) * high_count + holder // LOW) * n_grp + served_at // group_size
-    ) * share + rank % share
-    in_perm = sent_at[None, :] == request_ids[:, None]
-    my_start = ((seq_index % LOW) * high_count + seq_index // LOW) * row_share
-    my_rows = (
-        my_start + jnp.arange(row_share, dtype=jnp.int32)[:, None] == sent_at[None, :]
-    )
-    places = jnp.sum(jnp.where(my_rows[None], positions[:, None, :], 0), axis=2)
-    cosine, sine = rope_tables(places)
-    placed_at = served_at[None, :] == request_ids[:, None]
-    served_order = jnp.sum(jnp.where(placed_at, request_ids[None, :], 0), axis=1)
-    served_ids = lax.dynamic_slice_in_dim(served_order, grp_index * group_size, group_size, 0)
-    served_len = lengths[served_ids]
-    served_table = page_table[served_ids]
-    most_pages = page_table.shape[1]
-    page_counts = (served_len + PAGE - 1) // PAGE
-    logical = jnp.arange(most_pages, dtype=jnp.int32)
-    pool_pages = k_cache.shape[1] // PAGE
-    local_page = served_table - seq_index * pool_pages
-    usable = (
-        (logical[None, :] < page_counts[:, None]) & (local_page >= 0) & (local_page < pool_pages)
-    )
-    pool_ids = jnp.arange(pool_pages, dtype=jnp.int32)
-    matched = usable[:, :, None] & (local_page[:, :, None] == pool_ids[None, None, :])
-    owner_ids = jnp.arange(group_size, dtype=jnp.int32)
-    left = served_len[:, None] - logical[None, :] * PAGE
-    live = jnp.max(jnp.where(matched, left[:, :, None], 0), axis=(0, 1))
-    owner = jnp.max(jnp.where(matched, owner_ids[:, None, None], 0), axis=(0, 1))
-    back_at = served_at.reshape(high_count, LOW, row_share).transpose(1, 0, 2).reshape(-1)
-    out_perm = back_at[:, None] == request_ids[None, :]
+    n_seq, n_grp = lax.axis_size("seq"), lax.axis_size("grp")
+    cosine, sine = rope_tables(positions)
     return run_step(
-        n_seq, n_grp, owner, live, hidden, in_perm.astype(jnp.bfloat16),
-        out_perm.astype(jnp.bfloat16), b_qkv.reshape(-1, HD), cosine, sine, w_qkv, w_out, k_cache,
-        v_cache
+        n_seq, n_grp, hidden, group_of[None, :], lengths[None, :], page_table,
+        b_qkv.reshape(-1, HD), cosine, sine, w_qkv, w_out, k_cache, v_cache
     )
 
 

time: 129 us -> 117 us (0.907)
  Pallas kernels: 119 us -> 114 us
  other arithmetic: 5.07 us -> 2.03 us
  local copies, waits for them, and re-layouts: 3.82 us -> 1.58 us
    pallas_call x1, Pallas kernels: 119 us -> 114 us  [run_step(): pl.pallas_call(functools.partial(step_kernel, n_seq, n_grp), out_shape=ja...]
    gather x2 -> x0, local copies, waits for them, and re-layouts: 2.07 us -> none  [the longest x1 1.47 us: shards(): served_len = lengths[served_ids]]
    reduce_sum x3 -> x0, other arithmetic: 1.89 us -> none  [the longest x1 0.94 us: shards(): served_at = jnp.sum(before.astype(jnp.int32), axis=1)]
where the time goes in v3:
time: 117 us
  Pallas kernels  114 us (97%)
  other arithmetic  2.03 us (2%)
  local copies, waits for them, and re-layouts  1.58 us (1%)
    pallas_call x1, Pallas kernels, run_step(): pl.pallas_call(functools.partial(step_kernel, n_seq, n_grp), out_shape=ja...  114 us

profile of v3, /device:TPU:0, one launch (start us, length us, event | category | flops | bytes accessed | tf_op | source)
XLA Modules:
  0.0 117.3 jit_solution(1153499439858688196)
XLA Ops:
  0.0 0.7 convert_element_type.10
  0.7 1.3 %negate_select_fusion = (f32[256,128]{1,0:T(8,128)}, f32[256,128]{1,0:T(8,128)}) fusion(f32[128]{0:T(128)S(1)} %multiply_exponential_fusion, f32[256]{0:T(256)S(1)} %bitcast.8, f32[256]{0:T(256)S(1)} %bitcast.9, f32[256]{0:T(256)S(1)} %bitcast.7, pred[128]{0:T(512)(128)(4,1)S(1)} %get-tuple-element.10, pred[128]{0:T(512)(128)(4,1)S(1)} %get-tuple-element.11, ...), kind=kLoop, calls=%fused_computation | loop fusion | flops 163840 | bytes 266112 | tf_op jit(solution)/shard_map/jit(_where)/select_n | solution.py:653
  2.0 113.6 %shard_map.100 = bf16[32,2048]{1,0:T(8,128)(2,1)} custom-call(bf16[64,1024]{1,0:T(8,128)(2,1)} %hidden_ref.1, s32[1,256]{1,0:T(1,128)} %bitcast.10, s32[1,256]{1,0:T(1,128)} %bitcast.11, s32[256,128]{1,0:T(8,128)} %table_ref.1, f32[20,128]{1,0:T(8,128)} %bitcast.6, f32[256,128]{1,0:T(8,128)} %get-tuple-element.6.cos_all_ref, ...), custom_call_target="tpu_custom_call" | custom-call | flops 1342177280 | bytes 5242880 | tf_op jit(solution)/shard_map/pallas_call | solution.py:617
  115.7 1.6 %copy.12 = bf16[32,2048]{1,0:T(8,128)(2,1)} copy(bf16[32,2048]{1,0:T(8,128)(2,1)} %shard_map.100) | data formatting | bytes 262144
  (4 shorter events, 0.0 us)

commit v4 on v3

--- a/solution.py
+++ b/solution.py
@@ -34,14 +34,6 @@
 
 def greeted(n_seq, n_grp):
     pl.semaphore_wait(pltpu.get_barrier_semaphore(), n_seq + n_grp - 2)
-
-
-def split_exact(values):
-    terms = []
-    for _ in range(3):
-        terms.append(values.astype(jnp.bfloat16))
-        values = values - terms[-1].astype(jnp.float32)
-    return terms
 
 
 def row_col(shape):
@@ -74,7 +66,7 @@
     return served, sent
 
 
-def serve_tables(n_seq, n_grp, order, group_of_ref, len_ref, table_ref, cos_all_ref, sin_all_ref, back_ref,
+def serve_tables(n_seq, n_grp, order, group_of_ref, len_ref, table_ref, place_ref, back_ref,
                  cos_ref, sin_ref, slot_ref):
     served, sent = order
     seq, grp = lax.axis_index("seq"), lax.axis_index("grp")
@@ -93,12 +85,25 @@
 
     start = (lax.rem(seq, LOW) * high_count + seq // LOW) * row_share
     row, _ = row_col((row_share, total))
-    mine = one_hot(row + start.astype(jnp.float32) == sent)
-    for source, target in ((cos_all_ref, cos_ref), (sin_all_ref, sin_ref)):
-        target[...] = sum(
-            jnp.dot(mine, term, preferred_element_type=jnp.float32)
-            for term in split_exact(source[...])
-        )
+    mine = row + start.astype(jnp.float32) == sent
+    _, column = row_col((row_share, HD))
+    freq_index = column - jnp.where(column < HD // 2, 0.0, HD // 2)
+    inverse_freq = jnp.exp(freq_index * (-2.0 * math.log(rope_base) / HD))
+    spots = [
+        jnp.sum(
+            jnp.where(mine, place_ref[k : k + 1, :].astype(jnp.float32), 0.0), axis=1, keepdims=True
+        )
+        for k in range(3)
+    ]
+    chosen = jnp.where(
+        freq_index < HD // 8,
+        spots[0],
+        jnp.where(freq_index < HD // 8 + 3 * HD // 16, spots[1], spots[2]),
+    )
+    angles = chosen * inverse_freq
+    sine = jnp.sin(angles)
+    cos_ref[...] = jnp.cos(angles)
+    sin_ref[...] = jnp.where(column < HD // 2, -sine, sine)
 
     row = lax.broadcasted_iota(jnp.int32, (total, total), 0)
     col = lax.broadcasted_iota(jnp.int32, (total, total), 1)
@@ -253,7 +258,7 @@
 
 
 def step_kernel(n_seq, n_grp, hidden_ref, group_of_ref, len_ref, table_ref, bias_ref,
-                cos_all_ref, sin_all_ref, w_in_hbm, w_out_hbm, k_hbm, v_hbm, mixed_ref,
+                place_ref, w_in_hbm, w_out_hbm, k_hbm, v_hbm, mixed_ref,
                 perm_ref, back_ref, cos_ref, sin_ref, slot_ref, slots_ref,
                 key_ref, value_ref, w_in_ref, w_out_ref, hid_all, rows_ref, p_own, p_ys, p_yr,
                 p_zs, p_zr, turned_ref, d_send, d_recv, x_ref, wide_ref, block_ref, q_ref, nv_send,
@@ -302,7 +307,7 @@
     value_copy.start()
     for p in range(out_pieces):
         out_fetch(p).start()
-    serve_tables(n_seq, n_grp, order, group_of_ref, len_ref, table_ref, cos_all_ref, sin_all_ref, back_ref,
+    serve_tables(n_seq, n_grp, order, group_of_ref, len_ref, table_ref, place_ref, back_ref,
                  cos_ref, sin_ref, slot_ref)
     slot_copy = pltpu.make_async_copy(slot_ref, slots_ref, slot_sem)
     slot_copy.start()
@@ -540,7 +545,7 @@
         copy.wait_send()
 
 
-def run_step(n_seq, n_grp, hidden, group_of, lengths, table, bias, cosine, sine, w_qkv, w_out,
+def run_step(n_seq, n_grp, hidden, group_of, lengths, table, bias, places, w_qkv, w_out,
              k_cache, v_cache):
     group_size, depth = hidden.shape
     request_total = table.shape[0]
@@ -617,7 +622,7 @@
     return pl.pallas_call(
         functools.partial(step_kernel, n_seq, n_grp),
         out_shape=jax.ShapeDtypeStruct((row_share, out_cols), bf16),
-        in_specs=[vmem] * 7 + [hbm] * 4,
+        in_specs=[vmem] * 6 + [hbm] * 4,
         out_specs=vmem,
         scratch_shapes=[pltpu.VMEM(s, t) for s, t in scratch]
         + smem_scratch
@@ -632,33 +637,14 @@
             bytes_accessed=2 * depth * in_cols,
             transcendentals=0,
         ),
-    )(hidden, group_of, lengths, table, bias, cosine, sine, w_qkv, w_out, k_cache, v_cache)
-
-
-def rope_tables(positions):
-    column = jnp.arange(HD, dtype=jnp.int32)
-    freq_index = column % (HD // 2)
-    inverse_freq = jnp.exp(freq_index.astype(jnp.float32) * (-2.0 * math.log(rope_base) / HD))
-    section = jnp.where(
-        freq_index < HD // 8, 0, jnp.where(freq_index < HD // 8 + 3 * HD // 16, 1, 2)
-    )
-    place_float = positions.astype(jnp.float32)
-    chosen = jnp.where(
-        section[None, :] == 0,
-        place_float[0][:, None],
-        jnp.where(section[None, :] == 1, place_float[1][:, None], place_float[2][:, None]),
-    )
-    angles = chosen * inverse_freq[None, :]
-    sine = jnp.sin(angles)
-    return jnp.cos(angles), jnp.where((column < HD // 2)[None, :], -sine, sine)
+    )(hidden, group_of, lengths, table, bias, places, w_qkv, w_out, k_cache, v_cache)
 
 
 def shards(hidden, w_qkv, b_qkv, w_out, k_cache, v_cache, lengths, page_table, positions, group_of):
     n_seq, n_grp = lax.axis_size("seq"), lax.axis_size("grp")
-    cosine, sine = rope_tables(positions)
     return run_step(
         n_seq, n_grp, hidden, group_of[None, :], lengths[None, :], page_table,
-        b_qkv.reshape(-1, HD), cosine, sine, w_qkv, w_out, k_cache, v_cache
+        b_qkv.reshape(-1, HD), positions, w_qkv, w_out, k_cache, v_cache
     )
 
 

time: 117 us -> 115 us (0.983)
  other arithmetic: 2.03 us -> 0 us
    select_n x1 -> x0, other arithmetic: 1.32 us -> none  [rope_tables(): jnp.where((column < HD // 2)[None, :], -sine, sine)]
where the time goes in v4:
time: 115 us
  Pallas kernels  113 us (98%)
  local copies, waits for them, and re-layouts  1.57 us (1%)
    pallas_call x1, Pallas kernels, run_step(): pl.pallas_call(functools.partial(step_kernel, n_seq, n_grp), out_shape=ja...  113 us

profile of v4, /device:TPU:0, one launch (start us, length us, event | category | flops | bytes accessed | tf_op | source)
XLA Modules:
  0.0 115.0 jit_solution(13098606617429772210)
XLA Ops:
  0.0 113.5 %shard_map.100 = bf16[32,2048]{1,0:T(8,128)(2,1)} custom-call(bf16[64,1024]{1,0:T(8,128)(2,1)} %hidden_ref.1, s32[1,256]{1,0:T(1,128)} %bitcast.4, s32[1,256]{1,0:T(1,128)} %bitcast.5, s32[256,128]{1,0:T(8,128)} %table_ref.1, f32[20,128]{1,0:T(8,128)} %bitcast.3, s32[3,256]{1,0:T(4,128)} %place_ref.1, bf16[1024,2560]{1,0:T(8,128)(2,1)} %w_in_hbm.1, ...), custom_call_target="tpu_custom_call" | custom-call | flops 1342177280 | bytes 5242880 | tf_op jit(solution)/shard_map/pallas_call | solution.py:622
  113.5 1.6 %copy.12 = bf16[32,2048]{1,0:T(8,128)(2,1)} copy(bf16[32,2048]{1,0:T(8,128)(2,1)} %shard_map.100) | data formatting | bytes 262144
